TPU v7x, 32 devices: a whole 2x2x4 slice. The times are simulated.
32 devices in a mesh: lon: 16 (over z, x, core), lat: 2 (over y).
Axes of the slice: x: 2, y: 2, z: 4, core: 2. Of those that a mesh axis runs over, the one named last changes fastest.
Arguments:
- zonal_state: float32 [4, 32, 3, 8, 2048], P(None, None, None, 'lat', 'lon'), may hold values from -6 to 6
- zonal_courant: float32 [32, 8, 2048], P(None, 'lat', 'lon'), may hold values from -0.5 to 0.5
- zonal_length: int32 [8], P('lat'), may hold values from 512 to 2048, as said below
- zonal_owner: int32 [8, 2048], P('lat', 'lon'), may hold values from 0 to 63, as said below
- merid_state: float32 [4, 32, 3, 64, 256], P(None, None, None, 'lon', 'lat'), may hold values from -6 to 6
- merid_courant: float32 [32, 64, 256], P(None, 'lon', 'lat'), may hold values from -0.5 to 0.5
- mixing: float32 [4, 32, 32], replicated, may hold values from -0.18 to 0.18
Outputs:
- zonal_next: float32 [4, 32, 3, 8, 2048], P(None, None, None, 'lat', 'lon')
- merid_next: float32 [4, 32, 3, 64, 256], P(None, None, None, 'lon', 'lat')
- coupling: float32 [64, 8, 128], P('lon', 'lat')
Inputs may be any that keep to these rules, and one draw needn't show every extreme that they name: `zonal_owner`: non-decreasing along each row; each GCM column holds 16 to 48 consecutive cells of a row, and cell x belongs to a column g with |g - x // 32| <= 1. `zonal_length`: in each latitude sector (aligned blocks of 4 cycles) the first cycle holds 1088 cells and the second 2048.
All inputs are finite; a program needn't handle non-finite values.
Results may differ from a plain program's by a relative error of at most 0.0003.
Values sent between devices are 32-bit elements; how exact they have to be, the bound alone decides.
A program may use at most 64 MiB of HBM per device.

v0:
```python
import functools

import jax
import jax.numpy as jnp
from jax import lax
from jax.experimental import pallas as pl
from jax.experimental.pallas import tpu as pltpu
from jax.sharding import PartitionSpec as P

SUB = 4
GLON_DEV = 4
PAD = 8
MESH = pl.DeviceIdType.MESH
F32 = jnp.float32


def mix_into(products, at, fields, weights):
    wide = jnp.concatenate(fields, axis=0)
    high = wide.astype(jnp.bfloat16)
    low = (wide - high.astype(F32)).astype(jnp.bfloat16)
    out = jnp.dot(jnp.concatenate([high, low], axis=1), weights[...], preferred_element_type=F32)
    half = out.shape[1] // 2
    products[pl.ds(at, wide.shape[0]), :] = out[:, :half] + out[:, half:]


def updated(now, ahead, behind, courant, product):
    c_ahead = 0.3 - 0.5 * courant
    c_behind = 0.3 + 0.5 * courant
    x0, x1, x2 = now
    local = (0.3 * x0 + 0.1 * x1, 0.2 * x1 + 0.1 * (x0 + x2), 0.3 * x2 + 0.1 * x1)
    return [
        local[w] + c_ahead * ahead[w] + c_behind * behind[w] + product[w] for w in range(3)
    ]


def advance(src, dst, courants, products, weights, cells, rows_dev, ends):
    rows = 3 * cells
    step = 32
    for r in range(rows_dev):
        mix_into(
            products,
            r * rows,
            [src[w * 4 + r, pl.ds(PAD, cells), :] for w in range(3)],
            weights,
        )
    for r in range(rows_dev):
        for at in range(0, cells, step):
            now = [src[w * 4 + r, pl.ds(PAD + at, step), :] for w in range(3)]
            ahead = [src[w * 4 + r, pl.ds(PAD + at + 1, step), :] for w in range(3)]
            behind = [src[w * 4 + r, pl.ds(PAD + at - 1, step), :] for w in range(3)]
            courant = courants[12 + r, pl.ds(PAD + at, step), :]
            product = [
                products[pl.ds(r * rows + w * cells + at, step), :] for w in range(3)
            ]
            new = updated(now, ahead, behind, courant, product)
            for w in range(3):
                value = new[w]
                if ends is not None:
                    index = at + lax.broadcasted_iota(jnp.int32, (step, 128), 0)
                    value = jnp.where(index < ends[r], value, now[w])
                dst[w * 4 + r, pl.ds(PAD + at, step), :] = value


def advance_strips(first, second, products, weights, rows_dev):
    rows = 32 * rows_dev
    step = 32
    for t in range(SUB):
        src, dst = (first, second) if t % 2 == 0 else (second, first)
        mix_into(products, 0, [src[w, pl.ds(PAD, rows), :] for w in range(3)], weights)
        for at in range(0, rows, step):
            now = [src[w, pl.ds(PAD + at, step), :] for w in range(3)]
            ahead = [src[w, pl.ds(PAD + at + 1, step), :] for w in range(3)]
            behind = [src[w, pl.ds(PAD + at - 1, step), :] for w in range(3)]
            courant = first[3, pl.ds(PAD + at, step), :]
            product = [products[pl.ds(w * rows + at, step), :] for w in range(3)]
            new = updated(now, ahead, behind, courant, product)
            for w in range(3):
                dst[w, pl.ds(PAD + at, step), :] = new[w]


def load_state(state, field, courant, cells, rows_dev):
    for r in range(rows_dev):
        for w in range(3):
            at = w * rows_dev + r
            block = field[pl.ds(at, 128, stride=3 * rows_dev), :]
            state[w * 4 + r, pl.ds(PAD, cells), :] = block.T
        levels = courant[pl.ds(r, 32, stride=rows_dev), :]
        state[12 + r, pl.ds(PAD, cells), :] = jnp.concatenate([levels] * 4, axis=0).T


def store_state(out, state, cells, rows_dev):
    for r in range(rows_dev):
        for w in range(3):
            at = w * rows_dev + r
            out[pl.ds(at, 128, stride=3 * rows_dev), :] = state[w * 4 + r, pl.ds(PAD, cells), :].T


def pack_ends(first, last, state, cells, rows_dev):
    for r in range(rows_dev):
        for ch in range(4):
            put = pl.ds((r % 2) * 4, 4)
            first[r // 2, ch, put, :] = state[ch * 4 + r, pl.ds(PAD, 4), :]
            last[r // 2, ch, put, :] = state[ch * 4 + r, pl.ds(PAD + cells - 4, 4), :]


def kernel(
    n, n_lat, cells, rows_dev,
    len_hbm, z_hbm, zc_hbm, own_hbm, m_hbm, mc_hbm, mix_hbm,
    zs2, mo, co_ref,
    len_ref, z_ref, zc_ref, own_ref, m_ref, mc_ref, mix_ref, in_sems,
    zs, zs1, ms, ms1, ms2, mh, mh1, zh, zh1, products, weights,
    z_first, z_last, z_tail, m_first, m_last,
    from_left, from_right, heads, tails_in, tail_zero, m_halo, head_rows,
    c_left, c_right, c_from_left, c_from_right,
    sends, recvs, tail_sends, tail_recvs, head_sends,
    hello_next, hello_merid, hello_far,
):
    me = lax.axis_index("lon")
    lat = lax.axis_index("lat")
    right, left = lax.rem(me + 1, n), lax.rem(me + n - 1, n)
    partner = lax.rem(me + n // 2, n)
    wrap_from = n // 4 - 1
    mid = n // 2
    last = n - 1
    start = me * cells
    loads = [
        pltpu.make_async_copy(src, dst, in_sems.at[i])
        for i, (src, dst) in enumerate(
            (
                (z_hbm, z_ref), (zc_hbm, zc_ref), (len_hbm, len_ref), (m_hbm, m_ref),
                (mc_hbm, mc_ref), (mix_hbm, mix_ref), (own_hbm, own_ref),
            )
        )
    ]
    for load in loads:
        load.start()
    barrier = pltpu.get_barrier_semaphore()

    def greet(lon_to, lat_to):
        pl.semaphore_signal(barrier, inc=1, device_id=(lon_to, lat_to), device_id_type=MESH)

    def hello(semaphore, lon_to, lat_to):
        pl.semaphore_signal(semaphore, inc=1, device_id=(lon_to, lat_to), device_id_type=MESH)

    at_south, at_north = lat == 0, lat == n_lat - 1
    south_lon = jnp.where(at_south, partner, me)
    south_lat = jnp.where(at_south, 0, lat - 1)
    north_lon = jnp.where(at_north, partner, me)
    north_lat = jnp.where(at_north, n_lat - 1, lat + 1)
    south_slot = jnp.where(at_south, 0, 1)
    north_slot = jnp.where(at_north, 1, 0)
    is_hub, is_far, has_left, has_right = me == 0, me >= wrap_from, me > 0, me < last
    south_later = jnp.logical_and(at_south, me < mid)
    north_later = jnp.logical_or(jnp.logical_not(at_north), me < mid)
    south_earlier, north_earlier = jnp.logical_not(south_later), jnp.logical_not(north_later)

    @pl.when(has_right)
    def _():
        greet(right, lat)

    @pl.when(south_later)
    def _():
        greet(south_lon, south_lat)

    @pl.when(north_later)
    def _():
        greet(north_lon, north_lat)

    @pl.when(is_hub)
    def _():
        for j in range(wrap_from, n):
            greet(j, lat)

    one = lambda flag: jnp.where(flag, 1, 0)
    peers = one(has_left) + one(south_earlier) + one(north_earlier) + one(is_far)

    @pl.when(peers > 0)
    def _():
        pl.semaphore_wait(barrier, peers)

    @pl.when(is_far)
    def _():
        hello(hello_far.at[me], 0, lat)

    @pl.when(has_left)
    def _():
        hello(hello_next.at[0], left, lat)

    @pl.when(south_earlier)
    def _():
        hello(hello_merid.at[south_slot], south_lon, south_lat)

    @pl.when(north_earlier)
    def _():
        hello(hello_merid.at[north_slot], north_lon, north_lat)

    for load in loads[:3]:
        load.wait()
    load_state(zs, z_ref, zc_ref, cells, rows_dev)
    pack_ends(z_first, z_last, zs, cells, rows_dev)
    lengths = [len_ref[r] for r in range(rows_dev)]
    index8 = lax.broadcasted_iota(jnp.int32, (8, 128), 0)
    for r in range(rows_dev):
        at = jnp.clip(lengths[r] - 4 - start, -4, cells)
        cell = lengths[r] - 4 - start + index8
        own = (cell >= 0) & (cell < cells)
        for ch in range(4):
            value = zs[ch * 4 + r, pl.ds(PAD + at, 8), :]
            z_tail[r // 2, ch, pl.ds((r % 2) * 4, 4), :] = jnp.where(own, value, 0.0)[:4]

    def copy(src, dst, send, recv, lon_to, lat_to):
        return pltpu.make_async_remote_copy(
            src_ref=src, dst_ref=dst, send_sem=send, recv_sem=recv,
            device_id=(lon_to, lat_to), device_id_type=MESH,
        )

    def head_copy(j):
        return copy(z_first.at[1], heads.at[1], head_sends.at[j], recvs.at[4], j, lat)

    head_mid = copy(z_first.at[0], heads.at[0], sends.at[5], recvs.at[5], mid, lat)
    head_last = copy(z_first.at[0], from_right.at[0], sends.at[8], recvs.at[9], last, lat)
    tail_mid = copy(z_tail.at[0], tail_zero, sends.at[5], recvs.at[6], 0, lat)
    tail_last = copy(z_last.at[0], from_left.at[0], sends.at[8], recvs.at[9], 0, lat)

    def tail_copy(j):
        return copy(z_tail.at[1], tails_in.at[j], sends.at[4], tail_recvs.at[j], 0, lat)

    to_right = copy(z_last, from_left, sends.at[0], recvs.at[0], right, lat)
    to_left = copy(z_first, from_right, sends.at[1], recvs.at[1], left, lat)

    @pl.when(is_far)
    def _():
        tail_copy(me).start()

    @pl.when(me == mid)
    def _():
        tail_mid.start()

    @pl.when(me == last)
    def _():
        tail_last.start()

    @pl.when(has_left)
    def _():
        to_left.start()

    for load in loads[3:]:
        load.wait()
    load_state(ms, m_ref, mc_ref, cells, rows_dev)
    pack_ends(m_first, m_last, ms, cells, rows_dev)
    to_south = copy(
        m_first, m_halo.at[south_slot], sends.at[2], recvs.at[2 + south_slot], south_lon, south_lat
    )
    to_north = copy(
        m_last, m_halo.at[north_slot], sends.at[3], recvs.at[2 + north_slot], north_lon, north_lat
    )

    @pl.when(south_earlier)
    def _():
        to_south.start()

    @pl.when(north_earlier)
    def _():
        to_north.start()

    tiled = jnp.concatenate([mix_ref[...]] * 4, axis=1)
    block_of = lambda axis: lax.broadcasted_iota(jnp.int32, (128, 128), axis) // 32
    matrix = jnp.where(block_of(0) == block_of(1), tiled, 0.0).T
    w_high = matrix.astype(jnp.bfloat16)
    w_low = (matrix - w_high.astype(F32)).astype(jnp.bfloat16)
    pair = jnp.concatenate([w_high, w_low], axis=1)
    weights[pl.ds(0, 128), :] = pair
    weights[pl.ds(128, 128), :] = pair
    for buf in (zh, zh1, mh, mh1):
        for ch in range(3):
            buf[ch, pl.ds(0, 8), :] = jnp.zeros((8, 128), F32)
            buf[ch, pl.ds(PAD + 32 * rows_dev, 8), :] = jnp.zeros((8, 128), F32)

    @pl.when(has_right)
    def _():
        pl.semaphore_wait(hello_next.at[0], 1)
        to_right.start()

    def serve(low, high):
        @pl.when(is_hub)
        def _():
            for j in range(max(low, wrap_from), high):
                pl.semaphore_wait(hello_far.at[j], 1)
                head_copy(j).start()
                if j == mid:
                    head_mid.start()
                if j == last:
                    head_last.start()

    ends = [jnp.clip(lengths[r] - start, 0, cells) for r in range(rows_dev)]
    for src, dst in ((zs, zs1), (zs1, zs2), (zs2, zs1), (zs1, zs2)):
        advance(src, dst, zs, products, weights, cells, rows_dev, ends)
    serve(0, mid)

    @pl.when(north_later)
    def _():
        pl.semaphore_wait(hello_merid.at[1], 1)
        to_north.start()

    @pl.when(south_later)
    def _():
        pl.semaphore_wait(hello_merid.at[0], 1)
        to_south.start()

    for src, dst in ((ms, ms1), (ms1, ms2)):
        advance(src, dst, ms, products, weights, cells, rows_dev, None)
    serve(mid, mid + n // 4)
    for src, dst in ((ms2, ms1), (ms1, ms2)):
        advance(src, dst, ms, products, weights, cells, rows_dev, None)
    serve(mid + n // 4, n)

    copy(m_first, m_halo.at[0], sends.at[2], recvs.at[2], south_lon, south_lat).wait()
    copy(m_last, m_halo.at[1], sends.at[3], recvs.at[3], north_lon, north_lat).wait()
    for r in range(rows_dev):
        take = (r % 2) * 4
        for ch in range(4):
            turned = ch if ch == 3 else 2 - ch
            sign = -1.0 if ch == 3 else 1.0
            base = PAD + r * 32
            for j in range(4):
                plain = m_halo[0, r // 2, ch, pl.ds(take + j, 1), :]
                pole = sign * m_halo[0, r // 2, turned, pl.ds(take + 3 - j, 1), :]
                mh[ch, pl.ds(base + j, 1), :] = jnp.where(at_south, pole, plain)
                plain = m_halo[1, r // 2, ch, pl.ds(take + j, 1), :]
                pole = sign * m_halo[1, r // 2, turned, pl.ds(take + 3 - j, 1), :]
                mh[ch, pl.ds(base + 24 + j, 1), :] = jnp.where(at_north, pole, plain)
            mh[ch, pl.ds(base + 4, 12), :] = ms[ch * 4 + r, pl.ds(PAD, 12), :]
            mh[ch, pl.ds(base + 16, 8), :] = ms[ch * 4 + r, pl.ds(PAD + cells - 8, 8), :]
            mh[ch, pl.ds(base + 28, 4), :] = jnp.zeros((4, 128), F32)
    advance_strips(mh, mh1, products, weights, rows_dev)
    for r in range(rows_dev):
        for w in range(3):
            at, base = w * 4 + r, PAD + r * 32
            ms2[at, pl.ds(PAD, 4), :] = mh[w, pl.ds(base + 4, 4), :]
            ms2[at, pl.ds(PAD + cells - 4, 4), :] = mh[w, pl.ds(base + 20, 4), :]
    store_state(mo, ms2, cells, rows_dev)

    @pl.when(has_right)
    def _():
        to_right.wait_send()
        to_left_of_right = copy(z_first, from_right, sends.at[1], recvs.at[1], left, lat)
        to_left_of_right.wait_recv()

    @pl.when(has_left)
    def _():
        to_left.wait_send()
        to_right.wait_recv()

    @pl.when(is_far)
    def _():
        tail_copy(me).wait_send()
        head_copy(me).wait_recv()

    @pl.when(me == mid)
    def _():
        tail_mid.wait_send()
        head_mid.wait_recv()

    @pl.when(me == last)
    def _():
        tail_last.wait_send()
        head_last.wait_recv()

    @pl.when(is_hub)
    def _():
        for j in range(wrap_from, n):
            head_copy(j).wait_send()
            tail_copy(j).wait_recv()
        head_mid.wait_send()
        tail_mid.wait_recv()
        head_last.wait_send()
        tail_last.wait_recv()

    for r in range(rows_dev):
        take = pl.ds((r % 2) * 4, 4)
        for ch in range(4):
            zs[ch * 4 + r, pl.ds(PAD - 4, 4), :] = from_left[r // 2, ch, take, :]
            zs[ch * 4 + r, pl.ds(PAD + cells, 4), :] = from_right[r // 2, ch, take, :]

    @pl.when(is_hub)
    def _():
        for ch in range(4):
            zs[ch * 4, pl.ds(PAD - 4, 4), :] = tail_zero[ch, pl.ds(0, 4), :]
            total = tails_in[wrap_from, ch]
            for j in range(wrap_from + 1, n):
                total = total + tails_in[j, ch]
            for r in range(2, rows_dev):
                zs[ch * 4 + r, pl.ds(PAD - 4, 4), :] = total[(r % 2) * 4 : (r % 2) * 4 + 4]

    index16 = lax.broadcasted_iota(jnp.int32, (16, 128), 0)
    for r in range(rows_dev):
        room = lengths[r] - start
        end = ends[r]
        over = jnp.clip(room - cells, 0, 5)
        short = jnp.clip(room, 0, 12)
        for ch in range(4):
            upper = zs[ch * 4 + r, pl.ds(PAD + end - 8, 16), :]
            lower = zs[ch * 4 + r, pl.ds(PAD - 4, 16), :]
            if r != 1:
                head_rows[r, ch, pl.ds(16, 4), :] = heads[r // 2, ch, pl.ds((r % 2) * 4, 4), :]
                upper = jnp.where(
                    index16 - 8 >= over, head_rows[r, ch, pl.ds(8 - over, 16), :], upper
                )
                lower = jnp.where(
                    index16 - 4 >= short, head_rows[r, ch, pl.ds(12 - short, 16), :], lower
                )
            zh[ch, pl.ds(PAD + r * 32, 16), :] = lower
            zh[ch, pl.ds(PAD + r * 32 + 16, 16), :] = upper
    advance_strips(zh, zh1, products, weights, rows_dev)
    index4 = lax.broadcasted_iota(jnp.int32, (4, 128), 0)
    for r in range(rows_dev):
        base = PAD + r * 32
        for w in range(3):
            at = w * 4 + r
            low = zs2[at, pl.ds(PAD, 4), :]
            zs2[at, pl.ds(PAD, 4), :] = jnp.where(
                index4 < ends[r], zh[w, pl.ds(base + 4, 4), :], low
            )
        for block in range(0, cells, 8):
            ahead = block - ends[r]
            inside = (index8 + ahead >= -4) & (index8 + ahead < 0)
            take = base + 16 + jnp.clip(ahead + 8, -8, 8)
            for w in range(3):
                at = w * 4 + r
                high = zs2[at, pl.ds(PAD + block, 8), :]
                zs2[at, pl.ds(PAD + block, 8), :] = jnp.where(
                    inside, zh[w, pl.ds(take, 8), :], high
                )

    scale = GLON_DEV / (3.0 * cells)
    near = me * GLON_DEV - 1 + lax.broadcasted_iota(jnp.int32, (8, cells), 0)
    for r in range(rows_dev):
        body = pl.ds(PAD, cells)
        before = zs[r, body, :] + zs[4 + r, body, :] + zs[8 + r, body, :]
        after = zs2[r, body, :] + zs2[4 + r, body, :] + zs2[8 + r, body, :]
        delta = (after - before) * scale
        table = (own_ref[pl.ds(r, 1), :] == near).astype(F32)
        terms = jnp.dot(
            table, delta, precision=lax.Precision.HIGHEST, preferred_element_type=F32
        )
        c_left[pl.ds(r, 1), :] = terms[0:1]
        c_right[pl.ds(r, 1), :] = terms[GLON_DEV + 1 : GLON_DEV + 2]
        for g in range(GLON_DEV):
            co_ref[g, pl.ds(r, 1), :] = terms[g + 1 : g + 2]
    part_left = copy(c_left, c_from_right, sends.at[6], recvs.at[7], left, lat)
    part_right = copy(c_right, c_from_left, sends.at[7], recvs.at[8], right, lat)

    @pl.when(has_left)
    def _():
        part_left.start()

    @pl.when(has_right)
    def _():
        part_right.start()

    @pl.when(has_left)
    def _():
        part_left.wait_send()
        part_right.wait_recv()
        for r in range(rows_dev):
            co_ref[0, pl.ds(r, 1), :] += c_from_left[pl.ds(r, 1), :]

    @pl.when(has_right)
    def _():
        part_right.wait_send()
        part_left.wait_recv()
        for r in range(rows_dev):
            co_ref[GLON_DEV - 1, pl.ds(r, 1), :] += c_from_right[pl.ds(r, 1), :]


def finish(
    cells, rows_dev,
    zs, mo, co_in,
    zo_hbm, mo_hbm, co_hbm,
    zo, sems,
):
    mo_copy = pltpu.make_async_copy(mo, mo_hbm, sems.at[1])
    mo_copy.start()
    co_copy = pltpu.make_async_copy(co_in, co_hbm, sems.at[2])
    co_copy.start()
    store_state(zo, zs, cells, rows_dev)
    zo_copy = pltpu.make_async_copy(zo, zo_hbm, sems.at[0])
    zo_copy.start()
    mo_copy.wait()
    co_copy.wait()
    zo_copy.wait()


def solution(mesh):
    n, n_lat = mesh.shape["lon"], mesh.shape["lat"]

    def shards(
        zonal_state, zonal_courant, zonal_length, zonal_owner, merid_state, merid_courant, mixing
    ):
        nv, lev, wid, rows_dev, cells = zonal_state.shape
        flat = nv * lev * wid * rows_dev
        vmem = pl.BlockSpec(memory_space=pltpu.VMEM)
        hbm = pl.BlockSpec(memory_space=pltpu.HBM)
        shape = jax.ShapeDtypeStruct
        state = (16, cells + 2 * PAD, 128)
        strips = (4, 32 * rows_dev + 2 * PAD, 128)
        packet = pltpu.VMEM((2, 4, 8, 128), F32)
        small = pltpu.VMEM((8, 128), F32)
        products = pltpu.VMEM((rows_dev * 3 * cells, 128), F32)
        dma = pltpu.SemaphoreType.DMA
        regular = pltpu.SemaphoreType.REGULAR
        held = pl.pallas_call(
            functools.partial(kernel, n, n_lat, cells, rows_dev),
            out_shape=(
                shape(state, F32), shape((flat, cells), F32),
                shape((GLON_DEV, rows_dev, nv * lev), F32),
            ),
            in_specs=[hbm] * 7,
            out_specs=(vmem,) * 3,
            scratch_shapes=[
                pltpu.SMEM((rows_dev,), jnp.int32),
                pltpu.VMEM((flat, cells), F32),
                pltpu.VMEM((lev * rows_dev, cells), F32),
                pltpu.VMEM((rows_dev, cells), jnp.int32),
                pltpu.VMEM((flat, cells), F32),
                pltpu.VMEM((lev * rows_dev, cells), F32),
                pltpu.VMEM((nv * lev, lev), F32),
                dma((7,)),
                pltpu.VMEM(state, F32), pltpu.VMEM(state, F32),
                pltpu.VMEM(state, F32), pltpu.VMEM(state, F32), pltpu.VMEM(state, F32),
                pltpu.VMEM(strips, F32), pltpu.VMEM(strips, F32),
                pltpu.VMEM(strips, F32), pltpu.VMEM(strips, F32),
                products, pltpu.VMEM((256, 256), jnp.bfloat16),
                packet, packet, packet, packet, packet,
                packet, packet, packet,
                pltpu.VMEM((n, 4, 8, 128), F32),
                pltpu.VMEM((4, 8, 128), F32),
                pltpu.VMEM((2, 2, 4, 8, 128), F32),
                pltpu.VMEM((rows_dev, 4, 40, 128), F32),
                small, small, small, small,
                dma((9,)), dma((10,)), dma((1,)), dma((n,)), dma((n,)),
                regular((1,)), regular((2,)), regular((n,)),
            ],
            compiler_params=pltpu.CompilerParams(
                collective_id=0, has_side_effects=True, vmem_limit_bytes=48 * 1024 * 1024
            ),
        )(
            *(
                pltpu.with_memory_space_constraint(value, pltpu.HBM)
                for value in (
                    zonal_length,
                    zonal_state.reshape(flat, cells),
                    zonal_courant.reshape(lev * rows_dev, cells),
                    zonal_owner,
                    merid_state.reshape(flat, cells),
                    merid_courant.reshape(lev * rows_dev, cells),
                    mixing.reshape(nv * lev, lev),
                )
            )
        )
        zo, mo, co = pl.pallas_call(
            functools.partial(finish, cells, rows_dev),
            out_shape=(
                shape((flat, cells), F32), shape((flat, cells), F32),
                shape((GLON_DEV, rows_dev, nv * lev), F32),
            ),
            in_specs=[vmem] * 3,
            out_specs=(hbm,) * 3,
            scratch_shapes=[pltpu.VMEM((flat, cells), F32), dma((3,))],
            compiler_params=pltpu.CompilerParams(vmem_limit_bytes=40 * 1024 * 1024),
        )(*held)
        return zo.reshape(zonal_state.shape), mo.reshape(merid_state.shape), co

    return jax.shard_map(
        shards,
        mesh=mesh,
        in_specs=(
            P(None, None, None, "lat", "lon"),
            P(None, "lat", "lon"),
            P("lat"),
            P("lat", "lon"),
            P(None, None, None, "lon", "lat"),
            P(None, "lon", "lat"),
            P(),
        ),
        out_specs=(
            P(None, None, None, "lat", "lon"),
            P(None, None, None, "lon", "lat"),
            P("lon", "lat", None),
        ),
        check_vma=False,
    )
```

profile of v0, /device:TPU:1, one launch (start us, length us, event | category | flops | bytes accessed | tf_op | source)
XLA Modules:
  0.0 15.7 jit_solution(8941534687048300746)
XLA Ops:
  0.6 13.9 %shard_map.94 = (f32[16,144,128]{2,1,0:T(8,128)S(1)}, f32[1536,128]{1,0:T(8,128)S(1)}, f32[4,4,128]{2,1,0:T(4,128)S(1)}) custom-call(s32[4]{0:T(128)} %len_hbm.1, f32[1536,128]{1,0:T(8,128)} %bitcast.7, f32[128,128]{1,0:T(8,128)} %bitcast.9, s32[4,128]{1,0:T(4,128)} %own_hbm.1, f32[1536,128]{1,0:T(8,128)} %bitcast.8, f32[128,128]{1,0:T(8,128)} %bitcast.10, ...), custom_call_target="tpu_custom_call" | custom-call | tf_op jit(solution)/shard_map/pallas_call | solution.py:512
  14.6 1.2 %shard_map.95 = (f32[1536,128]{1,0:T(8,128)}, f32[1536,128]{1,0:T(8,128)}, f32[4,4,128]{2,1,0:T(4,128)}) custom-call(f32[16,144,128]{2,1,0:T(8,128)S(1)} %get-tuple-element.9.zs, f32[1536,128]{1,0:T(8,128)S(1)} %get-tuple-element.10.mo, f32[4,4,128]{2,1,0:T(4,128)S(1)} %get-tuple-element.11.co_in), custom_call_target="tpu_custom_call" | custom-call | tf_op jit(solution)/shard_map/pallas_call | solution.py:561
where the time goes:
time: 15.9 us; the launch traced here: 15.7 us
  Pallas kernels  15.1 us (95%)
  between operations  0.64 us (4%)
    pallas_call x1, Pallas kernels, shards(): pl.pallas_call(functools.partial(kernel, n, n_lat, cells, rows_dev), out_...  13.9 us
    pallas_call x1, Pallas kernels, shards(): pl.pallas_call(functools.partial(finish, cells, rows_dev), out_shape=(sha...  1.18 us

commit v1 on v0

--- a/solution.py
+++ b/solution.py
@@ -10,6 +10,8 @@
 SUB = 4
 GLON_DEV = 4
 PAD = 8
+STEP = 32
+UNSCALE = 10.0**-SUB
 MESH = pl.DeviceIdType.MESH
 F32 = jnp.float32
 
@@ -23,19 +25,19 @@
     products[pl.ds(at, wide.shape[0]), :] = out[:, :half] + out[:, half:]
 
 
-def updated(now, ahead, behind, courant, product):
-    c_ahead = 0.3 - 0.5 * courant
-    c_behind = 0.3 + 0.5 * courant
+def updated(now, ahead, behind, five, product):
+    c_ahead = 3.0 - five
+    c_behind = 3.0 + five
     x0, x1, x2 = now
-    local = (0.3 * x0 + 0.1 * x1, 0.2 * x1 + 0.1 * (x0 + x2), 0.3 * x2 + 0.1 * x1)
+    pairs = (x0 + x1, x0 + x2, x1 + x2)
     return [
-        local[w] + c_ahead * ahead[w] + c_behind * behind[w] + product[w] for w in range(3)
+        (pairs[w] + product[w]) + (c_ahead * ahead[w] + c_behind * behind[w]) for w in range(3)
     ]
 
 
-def advance(src, dst, courants, products, weights, cells, rows_dev, ends):
+def advance(src, dst, fives, products, weights, cells, rows_dev, ends, final=False):
     rows = 3 * cells
-    step = 32
+    step = STEP
     for r in range(rows_dev):
         mix_into(
             products,
@@ -48,22 +50,23 @@
             now = [src[w * 4 + r, pl.ds(PAD + at, step), :] for w in range(3)]
             ahead = [src[w * 4 + r, pl.ds(PAD + at + 1, step), :] for w in range(3)]
             behind = [src[w * 4 + r, pl.ds(PAD + at - 1, step), :] for w in range(3)]
-            courant = courants[12 + r, pl.ds(PAD + at, step), :]
+            five = fives[12 + r, pl.ds(PAD + at, step), :]
             product = [
                 products[pl.ds(r * rows + w * cells + at, step), :] for w in range(3)
             ]
-            new = updated(now, ahead, behind, courant, product)
+            new = updated(now, ahead, behind, five, product)
             for w in range(3):
-                value = new[w]
+                value = new[w] * UNSCALE if final else new[w]
                 if ends is not None:
                     index = at + lax.broadcasted_iota(jnp.int32, (step, 128), 0)
-                    value = jnp.where(index < ends[r], value, now[w])
+                    kept = fives[w * 4 + r, pl.ds(PAD + at, step), :]
+                    value = jnp.where(index < ends[r], value, kept)
                 dst[w * 4 + r, pl.ds(PAD + at, step), :] = value
 
 
 def advance_strips(first, second, products, weights, rows_dev):
     rows = 32 * rows_dev
-    step = 32
+    step = STEP
     for t in range(SUB):
         src, dst = (first, second) if t % 2 == 0 else (second, first)
         mix_into(products, 0, [src[w, pl.ds(PAD, rows), :] for w in range(3)], weights)
@@ -71,11 +74,11 @@
             now = [src[w, pl.ds(PAD + at, step), :] for w in range(3)]
             ahead = [src[w, pl.ds(PAD + at + 1, step), :] for w in range(3)]
             behind = [src[w, pl.ds(PAD + at - 1, step), :] for w in range(3)]
-            courant = first[3, pl.ds(PAD + at, step), :]
+            five = first[3, pl.ds(PAD + at, step), :]
             product = [products[pl.ds(w * rows + at, step), :] for w in range(3)]
-            new = updated(now, ahead, behind, courant, product)
+            new = updated(now, ahead, behind, five, product)
             for w in range(3):
-                dst[w, pl.ds(PAD + at, step), :] = new[w]
+                dst[w, pl.ds(PAD + at, step), :] = new[w] * UNSCALE if t == SUB - 1 else new[w]
 
 
 def load_state(state, field, courant, cells, rows_dev):
@@ -85,7 +88,7 @@
             block = field[pl.ds(at, 128, stride=3 * rows_dev), :]
             state[w * 4 + r, pl.ds(PAD, cells), :] = block.T
         levels = courant[pl.ds(r, 32, stride=rows_dev), :]
-        state[12 + r, pl.ds(PAD, cells), :] = jnp.concatenate([levels] * 4, axis=0).T
+        state[12 + r, pl.ds(PAD, cells), :] = jnp.concatenate([5.0 * levels] * 4, axis=0).T
 
 
 def store_state(out, state, cells, rows_dev):
@@ -106,14 +109,14 @@
 def kernel(
     n, n_lat, cells, rows_dev,
     len_hbm, z_hbm, zc_hbm, own_hbm, m_hbm, mc_hbm, mix_hbm,
-    zs2, mo, co_ref,
+    zo, mo, co_ref,
     len_ref, z_ref, zc_ref, own_ref, m_ref, mc_ref, mix_ref, in_sems,
-    zs, zs1, ms, ms1, ms2, mh, mh1, zh, zh1, products, weights,
+    zs, zs1, zs2, ms, ms1, ms2, mh, mh1, zh, zh1, products, weights,
     z_first, z_last, z_tail, m_first, m_last,
     from_left, from_right, heads, tails_in, tail_zero, m_halo, head_rows,
     c_left, c_right, c_from_left, c_from_right,
-    sends, recvs, tail_sends, tail_recvs, head_sends,
-    hello_next, hello_merid, hello_far,
+    sends, recvs, tail_recvs, head_sends,
+    hello_side, hello_merid, hello_far,
 ):
     me = lax.axis_index("lon")
     lat = lax.axis_index("lat")
@@ -154,9 +157,18 @@
     north_later = jnp.logical_or(jnp.logical_not(at_north), me < mid)
     south_earlier, north_earlier = jnp.logical_not(south_later), jnp.logical_not(north_later)
 
-    @pl.when(has_right)
+    odd = lax.rem(me, 2) == 1
+    even = lax.rem(me, 2) == 0
+    right_later, right_earlier = has_right & odd, has_right & even
+    left_later, left_earlier = has_left & odd, has_left & even
+
+    @pl.when(right_later)
     def _():
         greet(right, lat)
+
+    @pl.when(left_later)
+    def _():
+        greet(left, lat)
 
     @pl.when(south_later)
     def _():
@@ -172,7 +184,10 @@
             greet(j, lat)
 
     one = lambda flag: jnp.where(flag, 1, 0)
-    peers = one(has_left) + one(south_earlier) + one(north_earlier) + one(is_far)
+    peers = (
+        one(left_earlier) + one(right_earlier)
+        + one(south_earlier) + one(north_earlier) + one(is_far)
+    )
 
     @pl.when(peers > 0)
     def _():
@@ -180,11 +195,15 @@
 
     @pl.when(is_far)
     def _():
-        hello(hello_far.at[me], 0, lat)
-
-    @pl.when(has_left)
-    def _():
-        hello(hello_next.at[0], left, lat)
+        hello(hello_far.at[lax.div(me, n // 4)], 0, lat)
+
+    @pl.when(left_earlier)
+    def _():
+        hello(hello_side.at[1], left, lat)
+
+    @pl.when(right_earlier)
+    def _():
+        hello(hello_side.at[0], right, lat)
 
     @pl.when(south_earlier)
     def _():
@@ -215,7 +234,7 @@
         )
 
     def head_copy(j):
-        return copy(z_first.at[1], heads.at[1], head_sends.at[j], recvs.at[4], j, lat)
+        return copy(z_first.at[1], heads.at[1], head_sends.at[0], recvs.at[4], j, lat)
 
     head_mid = copy(z_first.at[0], heads.at[0], sends.at[5], recvs.at[5], mid, lat)
     head_last = copy(z_first.at[0], from_right.at[0], sends.at[8], recvs.at[9], last, lat)
@@ -223,26 +242,28 @@
     tail_last = copy(z_last.at[0], from_left.at[0], sends.at[8], recvs.at[9], 0, lat)
 
     def tail_copy(j):
-        return copy(z_tail.at[1], tails_in.at[j], sends.at[4], tail_recvs.at[j], 0, lat)
+        return copy(z_tail.at[1], tails_in.at[j], sends.at[4], tail_recvs.at[0], 0, lat)
 
     to_right = copy(z_last, from_left, sends.at[0], recvs.at[0], right, lat)
     to_left = copy(z_first, from_right, sends.at[1], recvs.at[1], left, lat)
 
-    @pl.when(is_far)
+    farthest = me >= last - n // 4 + 1
+
+    @pl.when(farthest)
     def _():
         tail_copy(me).start()
 
-    @pl.when(me == mid)
-    def _():
-        tail_mid.start()
-
     @pl.when(me == last)
     def _():
         tail_last.start()
 
-    @pl.when(has_left)
+    @pl.when(left_earlier)
     def _():
         to_left.start()
+
+    @pl.when(right_earlier)
+    def _():
+        to_right.start()
 
     for load in loads[3:]:
         load.wait()
@@ -263,29 +284,50 @@
     def _():
         to_north.start()
 
+    @pl.when(is_far & jnp.logical_not(farthest))
+    def _():
+        tail_copy(me).start()
+
+    @pl.when(me == mid)
+    def _():
+        tail_mid.start()
+
     tiled = jnp.concatenate([mix_ref[...]] * 4, axis=1)
-    block_of = lambda axis: lax.broadcasted_iota(jnp.int32, (128, 128), axis) // 32
+    index_of = lambda axis: lax.broadcasted_iota(jnp.int32, (128, 128), axis)
+    block_of = lambda axis: index_of(axis) // 32
     matrix = jnp.where(block_of(0) == block_of(1), tiled, 0.0).T
+    matrix = 10.0 * matrix + jnp.where(index_of(0) == index_of(1), 2.0, 0.0)
     w_high = matrix.astype(jnp.bfloat16)
     w_low = (matrix - w_high.astype(F32)).astype(jnp.bfloat16)
     pair = jnp.concatenate([w_high, w_low], axis=1)
     weights[pl.ds(0, 128), :] = pair
     weights[pl.ds(128, 128), :] = pair
+    for slot in range(16):
+        zs[slot, pl.ds(0, PAD), :] = jnp.zeros((PAD, 128), F32)
     for buf in (zh, zh1, mh, mh1):
         for ch in range(3):
             buf[ch, pl.ds(0, 8), :] = jnp.zeros((8, 128), F32)
             buf[ch, pl.ds(PAD + 32 * rows_dev, 8), :] = jnp.zeros((8, 128), F32)
 
-    @pl.when(has_right)
-    def _():
-        pl.semaphore_wait(hello_next.at[0], 1)
+    @pl.when(left_later)
+    def _():
+        pl.semaphore_wait(hello_side.at[0], 1)
+        to_left.start()
+
+    @pl.when(right_later)
+    def _():
+        pl.semaphore_wait(hello_side.at[1], 1)
         to_right.start()
 
-    def serve(low, high):
-        @pl.when(is_hub)
+    quarter = n // 4
+
+    def serve(group, now):
+        targets = [j for j in range(quarter * group, quarter * (group + 1)) if j >= wrap_from]
+
+        @pl.when(is_hub & now)
         def _():
-            for j in range(max(low, wrap_from), high):
-                pl.semaphore_wait(hello_far.at[j], 1)
+            pl.semaphore_wait(hello_far.at[group], len(targets))
+            for j in targets[::2] + targets[1::2]:
                 head_copy(j).start()
                 if j == mid:
                     head_mid.start()
@@ -293,26 +335,166 @@
                     head_last.start()
 
     ends = [jnp.clip(lengths[r] - start, 0, cells) for r in range(rows_dev)]
-    for src, dst in ((zs, zs1), (zs1, zs2), (zs2, zs1), (zs1, zs2)):
-        advance(src, dst, zs, products, weights, cells, rows_dev, ends)
-    serve(0, mid)
-
-    @pl.when(north_later)
-    def _():
-        pl.semaphore_wait(hello_merid.at[1], 1)
-        to_north.start()
-
-    @pl.when(south_later)
-    def _():
-        pl.semaphore_wait(hello_merid.at[0], 1)
-        to_south.start()
+    for src, dst in ((zs, zs1), (zs1, zs2), (zs2, zs1)):
+        advance(src, dst, zs, products, weights, cells, rows_dev, None)
+    advance(zs1, zs2, zs, products, weights, cells, rows_dev, ends, final=True)
+    always = me >= 0
+    serve(0, always)
+    serve(1, always)
+    serve(2, lat > 0)
+
+    def turn_poles():
+        @pl.when(north_later)
+        def _():
+            pl.semaphore_wait(hello_merid.at[1], 1)
+            to_north.start()
+
+        @pl.when(south_later)
+        def _():
+            pl.semaphore_wait(hello_merid.at[0], 1)
+            to_south.start()
+
+    @pl.when(me > 1)
+    def _():
+        turn_poles()
 
     for src, dst in ((ms, ms1), (ms1, ms2)):
         advance(src, dst, ms, products, weights, cells, rows_dev, None)
-    serve(mid, mid + n // 4)
+    @pl.when(me <= 1)
+    def _():
+        turn_poles()
+
+    serve(2, at_south)
+    serve(3, lat > 0)
     for src, dst in ((ms2, ms1), (ms1, ms2)):
-        advance(src, dst, ms, products, weights, cells, rows_dev, None)
-    serve(mid + n // 4, n)
+        advance(src, dst, ms, products, weights, cells, rows_dev, None, final=dst is ms2)
+    serve(3, at_south)
+
+    def fill_left():
+        for r in range(rows_dev):
+            take = pl.ds((r % 2) * 4, 4)
+            for ch in range(4):
+                zs[ch * 4 + r, pl.ds(PAD - 4, 4), :] = from_left[r // 2, ch, take, :]
+
+    def fill_right():
+        for r in range(rows_dev):
+            take = pl.ds((r % 2) * 4, 4)
+            for ch in range(4):
+                zs[ch * 4 + r, pl.ds(PAD + cells, 4), :] = from_right[r // 2, ch, take, :]
+
+    index16 = lax.broadcasted_iota(jnp.int32, (16, 128), 0)
+    index4 = lax.broadcasted_iota(jnp.int32, (4, 128), 0)
+
+    def seams():
+        for r in range(rows_dev):
+            room = lengths[r] - start
+            end = ends[r]
+            over = jnp.clip(room - cells, 0, 5)
+            short = jnp.clip(room, 0, 12)
+            for ch in range(4):
+                upper = zs[ch * 4 + r, pl.ds(PAD + end - 8, 16), :]
+                lower = zs[ch * 4 + r, pl.ds(PAD - 4, 16), :]
+                if r != 1:
+                    head_rows[r, ch, pl.ds(16, 4), :] = heads[
+                        r // 2, ch, pl.ds((r % 2) * 4, 4), :
+                    ]
+                    upper = jnp.where(
+                        index16 - 8 >= over, head_rows[r, ch, pl.ds(8 - over, 16), :], upper
+                    )
+                    lower = jnp.where(
+                        index16 - 4 >= short, head_rows[r, ch, pl.ds(12 - short, 16), :], lower
+                    )
+                zh[ch, pl.ds(PAD + r * 32, 16), :] = lower
+                zh[ch, pl.ds(PAD + r * 32 + 16, 16), :] = upper
+        advance_strips(zh, zh1, products, weights, rows_dev)
+        for r in range(rows_dev):
+            base = PAD + r * 32
+            for w in range(3):
+                at = w * 4 + r
+                low = zs2[at, pl.ds(PAD, 4), :]
+                zs2[at, pl.ds(PAD, 4), :] = jnp.where(
+                    index4 < ends[r], zh[w, pl.ds(base + 4, 4), :], low
+                )
+            for block in range(0, cells, 8):
+                ahead = block - ends[r]
+                inside = (index8 + ahead >= -4) & (index8 + ahead < 0)
+                take = base + 16 + jnp.clip(ahead + 8, -8, 8)
+                for w in range(3):
+                    at = w * 4 + r
+                    high = zs2[at, pl.ds(PAD + block, 8), :]
+                    zs2[at, pl.ds(PAD + block, 8), :] = jnp.where(
+                        inside, zh[w, pl.ds(take, 8), :], high
+                    )
+
+    scale = GLON_DEV / (3.0 * cells)
+    near = me * GLON_DEV - 1 + lax.broadcasted_iota(jnp.int32, (8, cells), 0)
+
+    def column_terms(r):
+        body = pl.ds(PAD, cells)
+        before = zs[r, body, :] + zs[4 + r, body, :] + zs[8 + r, body, :]
+        after = zs2[r, body, :] + zs2[4 + r, body, :] + zs2[8 + r, body, :]
+        delta = (after - before) * scale
+        high = delta.astype(jnp.bfloat16)
+        low = (delta - high.astype(F32)).astype(jnp.bfloat16)
+        table = (own_ref[pl.ds(r, 1), :] == near).astype(jnp.bfloat16)
+        both = jnp.dot(
+            table, jnp.concatenate([high, low], axis=1), preferred_element_type=F32
+        )
+        half = both.shape[1] // 2
+        return both[:, :half] + both[:, half:]
+
+    part_left = copy(c_left, c_from_right, sends.at[6], recvs.at[7], left, lat)
+    part_right = copy(c_right, c_from_left, sends.at[7], recvs.at[8], right, lat)
+
+    @pl.when(has_right)
+    def _():
+        to_right.wait_send()
+        to_left.wait_recv()
+
+    @pl.when(has_left)
+    def _():
+        to_left.wait_send()
+        to_right.wait_recv()
+
+    @pl.when(is_far)
+    def _():
+        tail_copy(me).wait_send()
+        head_copy(me).wait_recv()
+
+    @pl.when(me == mid)
+    def _():
+        tail_mid.wait_send()
+        head_mid.wait_recv()
+
+    @pl.when(me == last)
+    def _():
+        tail_last.wait_send()
+        head_last.wait_recv()
+
+    @pl.when(has_left)
+    def _():
+        fill_left()
+
+    fill_right()
+    seams()
+    for r in range(rows_dev):
+        terms = column_terms(r)
+        c_left[pl.ds(r, 1), :] = terms[0:1]
+        c_right[pl.ds(r, 1), :] = terms[GLON_DEV + 1 : GLON_DEV + 2]
+        for g in range(GLON_DEV):
+            co_ref[g, pl.ds(r, 1), :] = terms[g + 1 : g + 2]
+
+    @pl.when(has_left)
+    def _():
+        part_left.start()
+
+    @pl.when(has_right)
+    def _():
+        part_right.start()
+
+    @pl.when(has_left)
+    def _():
+        store_state(zo, zs2, cells, rows_dev)
 
     copy(m_first, m_halo.at[0], sends.at[2], recvs.at[2], south_lon, south_lat).wait()
     copy(m_last, m_halo.at[1], sends.at[3], recvs.at[3], north_lon, north_lat).wait()
@@ -340,50 +522,17 @@
             ms2[at, pl.ds(PAD + cells - 4, 4), :] = mh[w, pl.ds(base + 20, 4), :]
     store_state(mo, ms2, cells, rows_dev)
 
-    @pl.when(has_right)
-    def _():
-        to_right.wait_send()
-        to_left_of_right = copy(z_first, from_right, sends.at[1], recvs.at[1], left, lat)
-        to_left_of_right.wait_recv()
-
-    @pl.when(has_left)
-    def _():
-        to_left.wait_send()
-        to_right.wait_recv()
-
-    @pl.when(is_far)
-    def _():
-        tail_copy(me).wait_send()
-        head_copy(me).wait_recv()
-
-    @pl.when(me == mid)
-    def _():
-        tail_mid.wait_send()
-        head_mid.wait_recv()
-
-    @pl.when(me == last)
-    def _():
-        tail_last.wait_send()
-        head_last.wait_recv()
-
     @pl.when(is_hub)
     def _():
-        for j in range(wrap_from, n):
-            head_copy(j).wait_send()
-            tail_copy(j).wait_recv()
+        every = tails_in.at[pl.ds(wrap_from, n - wrap_from)]
+        all_far = copy(every, every, head_sends.at[0], tail_recvs.at[0], last, lat)
+        all_far.wait_send()
+        all_far.wait_recv()
         head_mid.wait_send()
         tail_mid.wait_recv()
         head_last.wait_send()
         tail_last.wait_recv()
-
-    for r in range(rows_dev):
-        take = pl.ds((r % 2) * 4, 4)
-        for ch in range(4):
-            zs[ch * 4 + r, pl.ds(PAD - 4, 4), :] = from_left[r // 2, ch, take, :]
-            zs[ch * 4 + r, pl.ds(PAD + cells, 4), :] = from_right[r // 2, ch, take, :]
-
-    @pl.when(is_hub)
-    def _():
+        fill_left()
         for ch in range(4):
             zs[ch * 4, pl.ds(PAD - 4, 4), :] = tail_zero[ch, pl.ds(0, 4), :]
             total = tails_in[wrap_from, ch]
@@ -391,72 +540,12 @@
                 total = total + tails_in[j, ch]
             for r in range(2, rows_dev):
                 zs[ch * 4 + r, pl.ds(PAD - 4, 4), :] = total[(r % 2) * 4 : (r % 2) * 4 + 4]
-
-    index16 = lax.broadcasted_iota(jnp.int32, (16, 128), 0)
-    for r in range(rows_dev):
-        room = lengths[r] - start
-        end = ends[r]
-        over = jnp.clip(room - cells, 0, 5)
-        short = jnp.clip(room, 0, 12)
-        for ch in range(4):
-            upper = zs[ch * 4 + r, pl.ds(PAD + end - 8, 16), :]
-            lower = zs[ch * 4 + r, pl.ds(PAD - 4, 16), :]
-            if r != 1:
-                head_rows[r, ch, pl.ds(16, 4), :] = heads[r // 2, ch, pl.ds((r % 2) * 4, 4), :]
-                upper = jnp.where(
-                    index16 - 8 >= over, head_rows[r, ch, pl.ds(8 - over, 16), :], upper
-                )
-                lower = jnp.where(
-                    index16 - 4 >= short, head_rows[r, ch, pl.ds(12 - short, 16), :], lower
-                )
-            zh[ch, pl.ds(PAD + r * 32, 16), :] = lower
-            zh[ch, pl.ds(PAD + r * 32 + 16, 16), :] = upper
-    advance_strips(zh, zh1, products, weights, rows_dev)
-    index4 = lax.broadcasted_iota(jnp.int32, (4, 128), 0)
-    for r in range(rows_dev):
-        base = PAD + r * 32
-        for w in range(3):
-            at = w * 4 + r
-            low = zs2[at, pl.ds(PAD, 4), :]
-            zs2[at, pl.ds(PAD, 4), :] = jnp.where(
-                index4 < ends[r], zh[w, pl.ds(base + 4, 4), :], low
-            )
-        for block in range(0, cells, 8):
-            ahead = block - ends[r]
-            inside = (index8 + ahead >= -4) & (index8 + ahead < 0)
-            take = base + 16 + jnp.clip(ahead + 8, -8, 8)
-            for w in range(3):
-                at = w * 4 + r
-                high = zs2[at, pl.ds(PAD + block, 8), :]
-                zs2[at, pl.ds(PAD + block, 8), :] = jnp.where(
-                    inside, zh[w, pl.ds(take, 8), :], high
-                )
-
-    scale = GLON_DEV / (3.0 * cells)
-    near = me * GLON_DEV - 1 + lax.broadcasted_iota(jnp.int32, (8, cells), 0)
-    for r in range(rows_dev):
-        body = pl.ds(PAD, cells)
-        before = zs[r, body, :] + zs[4 + r, body, :] + zs[8 + r, body, :]
-        after = zs2[r, body, :] + zs2[4 + r, body, :] + zs2[8 + r, body, :]
-        delta = (after - before) * scale
-        table = (own_ref[pl.ds(r, 1), :] == near).astype(F32)
-        terms = jnp.dot(
-            table, delta, precision=lax.Precision.HIGHEST, preferred_element_type=F32
-        )
-        c_left[pl.ds(r, 1), :] = terms[0:1]
-        c_right[pl.ds(r, 1), :] = terms[GLON_DEV + 1 : GLON_DEV + 2]
-        for g in range(GLON_DEV):
-            co_ref[g, pl.ds(r, 1), :] = terms[g + 1 : g + 2]
-    part_left = copy(c_left, c_from_right, sends.at[6], recvs.at[7], left, lat)
-    part_right = copy(c_right, c_from_left, sends.at[7], recvs.at[8], right, lat)
-
-    @pl.when(has_left)
-    def _():
-        part_left.start()
-
-    @pl.when(has_right)
-    def _():
-        part_right.start()
+        seams()
+        for r in range(rows_dev):
+            terms = column_terms(r)
+            for g in range(GLON_DEV):
+                co_ref[g, pl.ds(r, 1), :] = terms[g + 1 : g + 2]
+        store_state(zo, zs2, cells, rows_dev)
 
     @pl.when(has_left)
     def _():
@@ -473,22 +562,15 @@
             co_ref[GLON_DEV - 1, pl.ds(r, 1), :] += c_from_right[pl.ds(r, 1), :]
 
 
-def finish(
-    cells, rows_dev,
-    zs, mo, co_in,
-    zo_hbm, mo_hbm, co_hbm,
-    zo, sems,
-):
-    mo_copy = pltpu.make_async_copy(mo, mo_hbm, sems.at[1])
-    mo_copy.start()
-    co_copy = pltpu.make_async_copy(co_in, co_hbm, sems.at[2])
-    co_copy.start()
-    store_state(zo, zs, cells, rows_dev)
-    zo_copy = pltpu.make_async_copy(zo, zo_hbm, sems.at[0])
-    zo_copy.start()
-    mo_copy.wait()
-    co_copy.wait()
-    zo_copy.wait()
+def finish(zo, mo, co, zo_hbm, mo_hbm, co_hbm, sems):
+    copies = [
+        pltpu.make_async_copy(src, dst, sems.at[i])
+        for i, (src, dst) in enumerate(((zo, zo_hbm), (mo, mo_hbm), (co, co_hbm)))
+    ]
+    for out in copies:
+        out.start()
+    for out in copies:
+        out.wait()
 
 
 def solution(mesh):
@@ -512,7 +594,7 @@
         held = pl.pallas_call(
             functools.partial(kernel, n, n_lat, cells, rows_dev),
             out_shape=(
-                shape(state, F32), shape((flat, cells), F32),
+                shape((flat, cells), F32), shape((flat, cells), F32),
                 shape((GLON_DEV, rows_dev, nv * lev), F32),
             ),
             in_specs=[hbm] * 7,
@@ -526,7 +608,7 @@
                 pltpu.VMEM((lev * rows_dev, cells), F32),
                 pltpu.VMEM((nv * lev, lev), F32),
                 dma((7,)),
-                pltpu.VMEM(state, F32), pltpu.VMEM(state, F32),
+                pltpu.VMEM(state, F32), pltpu.VMEM(state, F32), pltpu.VMEM(state, F32),
                 pltpu.VMEM(state, F32), pltpu.VMEM(state, F32), pltpu.VMEM(state, F32),
                 pltpu.VMEM(strips, F32), pltpu.VMEM(strips, F32),
                 pltpu.VMEM(strips, F32), pltpu.VMEM(strips, F32),
@@ -538,8 +620,8 @@
                 pltpu.VMEM((2, 2, 4, 8, 128), F32),
                 pltpu.VMEM((rows_dev, 4, 40, 128), F32),
                 small, small, small, small,
-                dma((9,)), dma((10,)), dma((1,)), dma((n,)), dma((n,)),
-                regular((1,)), regular((2,)), regular((n,)),
+                dma((9,)), dma((10,)), dma((1,)), dma((1,)),
+                regular((2,)), regular((2,)), regular((4,)),
             ],
             compiler_params=pltpu.CompilerParams(
                 collective_id=0, has_side_effects=True, vmem_limit_bytes=48 * 1024 * 1024
@@ -559,14 +641,14 @@
             )
         )
         zo, mo, co = pl.pallas_call(
-            functools.partial(finish, cells, rows_dev),
+            finish,
             out_shape=(
                 shape((flat, cells), F32), shape((flat, cells), F32),
                 shape((GLON_DEV, rows_dev, nv * lev), F32),
             ),
             in_specs=[vmem] * 3,
             out_specs=(hbm,) * 3,
-            scratch_shapes=[pltpu.VMEM((flat, cells), F32), dma((3,))],
+            scratch_shapes=[dma((3,))],
             compiler_params=pltpu.CompilerParams(vmem_limit_bytes=40 * 1024 * 1024),
         )(*held)
         return zo.reshape(zonal_state.shape), mo.reshape(merid_state.shape), co

time: 15.9 us -> 14.2 us (0.89)
  the two profiles are of different devices: /device:TPU:1 before, /device:TPU:29 now
where the time goes in v1:
time: 14.2 us; the launch traced here: 14.1 us
  Pallas kernels  13.5 us (95%)
  between operations  0.64 us (5%)
    pallas_call x1, Pallas kernels, shards(): pl.pallas_call(functools.partial(kernel, n, n_lat, cells, rows_dev), out_...  12.3 us
    pallas_call x1, Pallas kernels, shards(): pl.pallas_call(finish, out_shape=(shape((flat, cells), F32), shape((flat,...  1.17 us

profile of v1, /device:TPU:29, one launch (start us, length us, event | category | flops | bytes accessed | tf_op | source)
XLA Modules:
  0.0 14.1 jit_solution(16092808624031631592)
XLA Ops:
  0.6 12.3 %shard_map.94 = (f32[1536,128]{1,0:T(8,128)S(1)}, f32[1536,128]{1,0:T(8,128)S(1)}, f32[4,4,128]{2,1,0:T(4,128)S(1)}) custom-call(s32[4]{0:T(128)} %len_hbm.1, f32[1536,128]{1,0:T(8,128)} %bitcast.7, f32[128,128]{1,0:T(8,128)} %bitcast.9, s32[4,128]{1,0:T(4,128)} %own_hbm.1, f32[1536,128]{1,0:T(8,128)} %bitcast.8, f32[128,128]{1,0:T(8,128)} %bitcast.10, ...), custom_call_target="tpu_custom_call" | custom-call | tf_op jit(solution)/shard_map/pallas_call | solution.py:594
  12.9 1.2 %shard_map.95 = (f32[1536,128]{1,0:T(8,128)}, f32[1536,128]{1,0:T(8,128)}, f32[4,4,128]{2,1,0:T(4,128)}) custom-call(f32[1536,128]{1,0:T(8,128)S(1)} %get-tuple-element.9.zo, f32[1536,128]{1,0:T(8,128)S(1)} %get-tuple-element.10.mo, f32[4,4,128]{2,1,0:T(4,128)S(1)} %get-tuple-element.11.co), custom_call_target="tpu_custom_call" | custom-call | tf_op jit(solution)/shard_map/pallas_call | solution.py:643

commit v2 on v1

--- a/solution.py
+++ b/solution.py
@@ -64,8 +64,7 @@
                 dst[w * 4 + r, pl.ds(PAD + at, step), :] = value
 
 
-def advance_strips(first, second, products, weights, rows_dev):
-    rows = 32 * rows_dev
+def advance_strips(first, second, products, weights, rows):
     step = STEP
     for t in range(SUB):
         src, dst = (first, second) if t % 2 == 0 else (second, first)
@@ -111,9 +110,10 @@
     len_hbm, z_hbm, zc_hbm, own_hbm, m_hbm, mc_hbm, mix_hbm,
     zo, mo, co_ref,
     len_ref, z_ref, zc_ref, own_ref, m_ref, mc_ref, mix_ref, in_sems,
-    zs, zs1, zs2, ms, ms1, ms2, mh, mh1, zh, zh1, products, weights,
+    zs, zs1, zs2, ms, ms1, ms2, fh, fh1, zh, zh1, products, weights,
     z_first, z_last, z_tail, m_first, m_last,
-    from_left, from_right, heads, tails_in, tail_zero, m_halo, head_rows,
+    from_left, from_right, heads, tails_in, tail_zero, m_halo,
+    z_window, w_left, w_right, seam_owner,
     c_left, c_right, c_from_left, c_from_right,
     sends, recvs, tail_recvs, head_sends,
     hello_side, hello_merid, hello_far,
@@ -237,7 +237,7 @@
         return copy(z_first.at[1], heads.at[1], head_sends.at[0], recvs.at[4], j, lat)
 
     head_mid = copy(z_first.at[0], heads.at[0], sends.at[5], recvs.at[5], mid, lat)
-    head_last = copy(z_first.at[0], from_right.at[0], sends.at[8], recvs.at[9], last, lat)
+    head_last = copy(z_first.at[0], heads.at[0], sends.at[8], recvs.at[9], last, lat)
     tail_mid = copy(z_tail.at[0], tail_zero, sends.at[5], recvs.at[6], 0, lat)
     tail_last = copy(z_last.at[0], from_left.at[0], sends.at[8], recvs.at[9], 0, lat)
 
@@ -247,11 +247,13 @@
     to_right = copy(z_last, from_left, sends.at[0], recvs.at[0], right, lat)
     to_left = copy(z_first, from_right, sends.at[1], recvs.at[1], left, lat)
 
-    farthest = me >= last - n // 4 + 1
-
-    @pl.when(farthest)
+    @pl.when(is_far)
     def _():
         tail_copy(me).start()
+
+    @pl.when(me == mid)
+    def _():
+        tail_mid.start()
 
     @pl.when(me == last)
     def _():
@@ -276,21 +278,20 @@
         m_last, m_halo.at[north_slot], sends.at[3], recvs.at[2 + north_slot], north_lon, north_lat
     )
 
-    @pl.when(south_earlier)
+    def over_poles(some):
+        @pl.when(at_south & some)
+        def _():
+            to_south.start()
+
+        @pl.when(at_north & some)
+        def _():
+            to_north.start()
+
+    @pl.when(jnp.logical_not(at_south))
     def _():
         to_south.start()
 
-    @pl.when(north_earlier)
-    def _():
-        to_north.start()
-
-    @pl.when(is_far & jnp.logical_not(farthest))
-    def _():
-        tail_copy(me).start()
-
-    @pl.when(me == mid)
-    def _():
-        tail_mid.start()
+    over_poles((me >= mid) & (me < mid + 2))
 
     tiled = jnp.concatenate([mix_ref[...]] * 4, axis=1)
     index_of = lambda axis: lax.broadcasted_iota(jnp.int32, (128, 128), axis)
@@ -302,12 +303,14 @@
     pair = jnp.concatenate([w_high, w_low], axis=1)
     weights[pl.ds(0, 128), :] = pair
     weights[pl.ds(128, 128), :] = pair
+    zeros = jnp.zeros((PAD, 128), F32)
     for slot in range(16):
-        zs[slot, pl.ds(0, PAD), :] = jnp.zeros((PAD, 128), F32)
-    for buf in (zh, zh1, mh, mh1):
+        zs[slot, pl.ds(0, PAD), :] = zeros
+        zs[slot, pl.ds(PAD + cells, PAD), :] = zeros
+    for buf in (zh, zh1, fh, fh1):
         for ch in range(3):
-            buf[ch, pl.ds(0, 8), :] = jnp.zeros((8, 128), F32)
-            buf[ch, pl.ds(PAD + 32 * rows_dev, 8), :] = jnp.zeros((8, 128), F32)
+            buf[ch, pl.ds(0, PAD), :] = zeros
+            buf[ch, pl.ds(buf.shape[1] - PAD, PAD), :] = zeros
 
     @pl.when(left_later)
     def _():
@@ -343,32 +346,53 @@
     serve(1, always)
     serve(2, lat > 0)
 
-    def turn_poles():
-        @pl.when(north_later)
+    @pl.when(jnp.logical_not(at_north))
+    def _():
+        pl.semaphore_wait(hello_merid.at[1], 1)
+        to_north.start()
+
+    def ready_poles(some):
+        @pl.when(at_south & some)
+        def _():
+            pl.semaphore_wait(hello_merid.at[0], 1)
+
+        @pl.when(at_north & some)
         def _():
             pl.semaphore_wait(hello_merid.at[1], 1)
-            to_north.start()
-
-        @pl.when(south_later)
-        def _():
-            pl.semaphore_wait(hello_merid.at[0], 1)
-            to_south.start()
-
-    @pl.when(me > 1)
-    def _():
-        turn_poles()
+
+    ready_poles((me > 1) & (me < mid))
+    over_poles((me > 1) & ((me < mid) | (me >= mid + 2)))
+
+    for r in range(rows_dev):
+        owners = (own_ref[pl.ds(r, 1), :] + 1).astype(F32)
+        zs[16 + r, pl.ds(PAD, cells), :] = jnp.broadcast_to(owners, (128, cells)).T
+    for r in range(rows_dev):
+        at = jnp.clip(lengths[r] - 8 - start, -8, cells)
+        cell = lengths[r] - 8 - start + index8
+        for ch in range(5):
+            value = zs[ch * 4 + r, pl.ds(PAD + at, 8), :]
+            z_window[r, ch, :, :] = jnp.where((cell >= 0) & (cell < cells), value, 0.0)
+    moving = z_window.at[pl.ds(2, rows_dev - 2)]
+    window_left = copy(moving, w_right, sends.at[9], recvs.at[10], left, lat)
+    window_right = copy(moving, w_left, sends.at[10], recvs.at[11], right, lat)
+
+    @pl.when(has_left)
+    def _():
+        window_left.start()
+
+    @pl.when(has_right)
+    def _():
+        window_right.start()
 
     for src, dst in ((ms, ms1), (ms1, ms2)):
         advance(src, dst, ms, products, weights, cells, rows_dev, None)
-    @pl.when(me <= 1)
-    def _():
-        turn_poles()
-
     serve(2, at_south)
     serve(3, lat > 0)
     for src, dst in ((ms2, ms1), (ms1, ms2)):
         advance(src, dst, ms, products, weights, cells, rows_dev, None, final=dst is ms2)
     serve(3, at_south)
+    ready_poles(me <= 1)
+    over_poles(me <= 1)
 
     def fill_left():
         for r in range(rows_dev):
@@ -382,52 +406,13 @@
             for ch in range(4):
                 zs[ch * 4 + r, pl.ds(PAD + cells, 4), :] = from_right[r // 2, ch, take, :]
 
-    index16 = lax.broadcasted_iota(jnp.int32, (16, 128), 0)
     index4 = lax.broadcasted_iota(jnp.int32, (4, 128), 0)
-
-    def seams():
-        for r in range(rows_dev):
-            room = lengths[r] - start
-            end = ends[r]
-            over = jnp.clip(room - cells, 0, 5)
-            short = jnp.clip(room, 0, 12)
-            for ch in range(4):
-                upper = zs[ch * 4 + r, pl.ds(PAD + end - 8, 16), :]
-                lower = zs[ch * 4 + r, pl.ds(PAD - 4, 16), :]
-                if r != 1:
-                    head_rows[r, ch, pl.ds(16, 4), :] = heads[
-                        r // 2, ch, pl.ds((r % 2) * 4, 4), :
-                    ]
-                    upper = jnp.where(
-                        index16 - 8 >= over, head_rows[r, ch, pl.ds(8 - over, 16), :], upper
-                    )
-                    lower = jnp.where(
-                        index16 - 4 >= short, head_rows[r, ch, pl.ds(12 - short, 16), :], lower
-                    )
-                zh[ch, pl.ds(PAD + r * 32, 16), :] = lower
-                zh[ch, pl.ds(PAD + r * 32 + 16, 16), :] = upper
-        advance_strips(zh, zh1, products, weights, rows_dev)
-        for r in range(rows_dev):
-            base = PAD + r * 32
-            for w in range(3):
-                at = w * 4 + r
-                low = zs2[at, pl.ds(PAD, 4), :]
-                zs2[at, pl.ds(PAD, 4), :] = jnp.where(
-                    index4 < ends[r], zh[w, pl.ds(base + 4, 4), :], low
-                )
-            for block in range(0, cells, 8):
-                ahead = block - ends[r]
-                inside = (index8 + ahead >= -4) & (index8 + ahead < 0)
-                take = base + 16 + jnp.clip(ahead + 8, -8, 8)
-                for w in range(3):
-                    at = w * 4 + r
-                    high = zs2[at, pl.ds(PAD + block, 8), :]
-                    zs2[at, pl.ds(PAD + block, 8), :] = jnp.where(
-                        inside, zh[w, pl.ds(take, 8), :], high
-                    )
 
     scale = GLON_DEV / (3.0 * cells)
     near = me * GLON_DEV - 1 + lax.broadcasted_iota(jnp.int32, (8, cells), 0)
+    lane = lax.broadcasted_iota(jnp.int32, (8, cells), 1)
+
+    first_late = jnp.where(is_hub, 4, 0)
 
     def column_terms(r):
         body = pl.ds(PAD, cells)
@@ -436,7 +421,9 @@
         delta = (after - before) * scale
         high = delta.astype(jnp.bfloat16)
         low = (delta - high.astype(F32)).astype(jnp.bfloat16)
-        table = (own_ref[pl.ds(r, 1), :] == near).astype(jnp.bfloat16)
+        to_end = lane - (lengths[r] - start)
+        early = ((to_end < -4) | (to_end >= 0)) & (lane >= first_late)
+        table = ((own_ref[pl.ds(r, 1), :] == near) & early).astype(jnp.bfloat16)
         both = jnp.dot(
             table, jnp.concatenate([high, low], axis=1), preferred_element_type=F32
         )
@@ -456,27 +443,28 @@
         to_left.wait_send()
         to_right.wait_recv()
 
-    @pl.when(is_far)
-    def _():
-        tail_copy(me).wait_send()
-        head_copy(me).wait_recv()
-
-    @pl.when(me == mid)
-    def _():
-        tail_mid.wait_send()
-        head_mid.wait_recv()
-
-    @pl.when(me == last)
-    def _():
-        tail_last.wait_send()
-        head_last.wait_recv()
-
     @pl.when(has_left)
     def _():
         fill_left()
 
-    fill_right()
-    seams()
+    @pl.when(has_right)
+    def _():
+        fill_right()
+
+    for r in range(rows_dev):
+        for ch in range(4):
+            base = PAD + r * 32
+            zh[ch, pl.ds(base, 16), :] = zs[ch * 4 + r, pl.ds(PAD - 4, 16), :]
+            zh[ch, pl.ds(base + 16, 16), :] = zs[ch * 4 + r, pl.ds(PAD + cells - 8, 16), :]
+    advance_strips(zh, zh1, products, weights, 32 * rows_dev)
+    for r in range(rows_dev):
+        base = PAD + r * 32
+        for w in range(3):
+            for cell, take in ((0, base + 4), (cells - 4, base + 20)):
+                old = zs2[w * 4 + r, pl.ds(PAD + cell, 4), :]
+                zs2[w * 4 + r, pl.ds(PAD + cell, 4), :] = jnp.where(
+                    index4 + cell < ends[r], zh[w, pl.ds(take, 4), :], old
+                )
     for r in range(rows_dev):
         terms = column_terms(r)
         c_left[pl.ds(r, 1), :] = terms[0:1]
@@ -492,35 +480,33 @@
     def _():
         part_right.start()
 
-    @pl.when(has_left)
-    def _():
-        store_state(zo, zs2, cells, rows_dev)
-
     copy(m_first, m_halo.at[0], sends.at[2], recvs.at[2], south_lon, south_lat).wait()
     copy(m_last, m_halo.at[1], sends.at[3], recvs.at[3], north_lon, north_lat).wait()
-    for r in range(rows_dev):
-        take = (r % 2) * 4
-        for ch in range(4):
-            turned = ch if ch == 3 else 2 - ch
-            sign = -1.0 if ch == 3 else 1.0
-            base = PAD + r * 32
-            for j in range(4):
-                plain = m_halo[0, r // 2, ch, pl.ds(take + j, 1), :]
-                pole = sign * m_halo[0, r // 2, turned, pl.ds(take + 3 - j, 1), :]
-                mh[ch, pl.ds(base + j, 1), :] = jnp.where(at_south, pole, plain)
-                plain = m_halo[1, r // 2, ch, pl.ds(take + j, 1), :]
-                pole = sign * m_halo[1, r // 2, turned, pl.ds(take + 3 - j, 1), :]
-                mh[ch, pl.ds(base + 24 + j, 1), :] = jnp.where(at_north, pole, plain)
-            mh[ch, pl.ds(base + 4, 12), :] = ms[ch * 4 + r, pl.ds(PAD, 12), :]
-            mh[ch, pl.ds(base + 16, 8), :] = ms[ch * 4 + r, pl.ds(PAD + cells - 8, 8), :]
-            mh[ch, pl.ds(base + 28, 4), :] = jnp.zeros((4, 128), F32)
-    advance_strips(mh, mh1, products, weights, rows_dev)
-    for r in range(rows_dev):
-        for w in range(3):
-            at, base = w * 4 + r, PAD + r * 32
-            ms2[at, pl.ds(PAD, 4), :] = mh[w, pl.ds(base + 4, 4), :]
-            ms2[at, pl.ds(PAD + cells - 4, 4), :] = mh[w, pl.ds(base + 20, 4), :]
-    store_state(mo, ms2, cells, rows_dev)
+
+    @pl.when(is_far)
+    def _():
+        tail_copy(me).wait_send()
+        head_copy(me).wait_recv()
+
+    @pl.when(me == mid)
+    def _():
+        tail_mid.wait_send()
+        head_mid.wait_recv()
+
+    @pl.when(me == last)
+    def _():
+        tail_last.wait_send()
+        head_last.wait_recv()
+
+    @pl.when(has_left)
+    def _():
+        window_left.wait_send()
+        window_right.wait_recv()
+
+    @pl.when(has_right)
+    def _():
+        window_right.wait_send()
+        window_left.wait_recv()
 
     @pl.when(is_hub)
     def _():
@@ -532,20 +518,99 @@
         tail_mid.wait_recv()
         head_last.wait_send()
         tail_last.wait_recv()
-        fill_left()
+
+    @pl.when(is_hub)
+    def _():
         for ch in range(4):
-            zs[ch * 4, pl.ds(PAD - 4, 4), :] = tail_zero[ch, pl.ds(0, 4), :]
             total = tails_in[wrap_from, ch]
             for j in range(wrap_from + 1, n):
                 total = total + tails_in[j, ch]
+            fh[ch, pl.ds(PAD, 4), :] = tail_zero[ch, pl.ds(0, 4), :]
+            fh[ch, pl.ds(PAD + 16, 4), :] = from_left[0, ch, pl.ds(4, 4), :]
             for r in range(2, rows_dev):
-                zs[ch * 4 + r, pl.ds(PAD - 4, 4), :] = total[(r % 2) * 4 : (r % 2) * 4 + 4]
-        seams()
+                half = (r % 2) * 4
+                fh[ch, pl.ds(PAD + 16 * r, 4), :] = total[half : half + 4]
+            for r in range(rows_dev):
+                fh[ch, pl.ds(PAD + 16 * r + 4, 12), :] = zs[ch * 4 + r, pl.ds(PAD, 12), :]
         for r in range(rows_dev):
-            terms = column_terms(r)
-            for g in range(GLON_DEV):
-                co_ref[g, pl.ds(r, 1), :] = terms[g + 1 : g + 2]
-        store_state(zo, zs2, cells, rows_dev)
+            seam_owner[r, :, :] = zs[16 + r, pl.ds(PAD, 8), :]
+
+    @pl.when(has_left)
+    def _():
+        for r in range(rows_dev):
+            for ch in range(5):
+                window = z_window[r, ch]
+                if r >= 2:
+                    window = window + w_left[r - 2, ch]
+                    window = window + jnp.where(has_right, w_right[r - 2, ch], 0.0)
+                if ch == 4:
+                    seam_owner[r, pl.ds(0, 4), :] = window[4:8]
+                    continue
+                base = PAD + 16 * r
+                fh[ch, pl.ds(base, 8), :] = window
+                fh[ch, pl.ds(base + 8, 4), :] = heads[r // 2, ch, pl.ds((r % 2) * 4, 4), :]
+                fh[ch, pl.ds(base + 12, 4), :] = jnp.zeros((4, 128), F32)
+
+    merid = PAD + 16 * rows_dev
+    for r in range(rows_dev):
+        take = (r % 2) * 4
+        for ch in range(4):
+            turned = ch if ch == 3 else 2 - ch
+            sign = -1.0 if ch == 3 else 1.0
+            base = merid + r * 32
+            for j in range(4):
+                plain = m_halo[0, r // 2, ch, pl.ds(take + j, 1), :]
+                pole = sign * m_halo[0, r // 2, turned, pl.ds(take + 3 - j, 1), :]
+                fh[ch, pl.ds(base + j, 1), :] = jnp.where(at_south, pole, plain)
+                plain = m_halo[1, r // 2, ch, pl.ds(take + j, 1), :]
+                pole = sign * m_halo[1, r // 2, turned, pl.ds(take + 3 - j, 1), :]
+                fh[ch, pl.ds(base + 24 + j, 1), :] = jnp.where(at_north, pole, plain)
+            fh[ch, pl.ds(base + 4, 12), :] = ms[ch * 4 + r, pl.ds(PAD, 12), :]
+            fh[ch, pl.ds(base + 16, 8), :] = ms[ch * 4 + r, pl.ds(PAD + cells - 8, 8), :]
+            fh[ch, pl.ds(base + 28, 4), :] = jnp.zeros((4, 128), F32)
+
+    def wanted(r):
+        at = pl.ds(PAD + 16 * r + 4, 4)
+        return fh[0, at, :] + fh[1, at, :] + fh[2, at, :]
+
+    seam_before = [wanted(r) for r in range(rows_dev)]
+    advance_strips(fh, fh1, products, weights, 48 * rows_dev)
+    for r in range(rows_dev):
+        for w in range(3):
+            at, base = w * 4 + r, merid + r * 32
+            ms2[at, pl.ds(PAD, 4), :] = fh[w, pl.ds(base + 4, 4), :]
+            ms2[at, pl.ds(PAD + cells - 4, 4), :] = fh[w, pl.ds(base + 20, 4), :]
+    store_state(mo, ms2, cells, rows_dev)
+
+    @pl.when(is_hub)
+    def _():
+        for r in range(rows_dev):
+            for w in range(3):
+                zs2[w * 4 + r, pl.ds(PAD, 4), :] = fh[w, pl.ds(PAD + 16 * r + 4, 4), :]
+
+    @pl.when(has_left)
+    def _():
+        for r in range(rows_dev):
+            for block in range(0, cells, 8):
+                ahead = block - (lengths[r] - start)
+                inside = (index8 + ahead >= -4) & (index8 + ahead < 0)
+                take = PAD + 16 * r + 8 + jnp.clip(ahead, -12, 0)
+                for w in range(3):
+                    at = w * 4 + r
+                    old = zs2[at, pl.ds(PAD + block, 8), :]
+                    zs2[at, pl.ds(PAD + block, 8), :] = jnp.where(
+                        inside, fh[w, pl.ds(take, 8), :], old
+                    )
+
+    store_state(zo, zs2, cells, rows_dev)
+    for r in range(rows_dev):
+        delta = (wanted(r) - seam_before[r]) * scale
+        owner = seam_owner[r, pl.ds(0, 4), :]
+        for g in range(GLON_DEV):
+            mine = owner == (me * GLON_DEV + g + 1).astype(F32)
+            co_ref[g, pl.ds(r, 1), :] += jnp.sum(
+                jnp.where(mine, delta, 0.0), axis=0, keepdims=True
+            )
 
     @pl.when(has_left)
     def _():
@@ -608,9 +673,11 @@
                 pltpu.VMEM((lev * rows_dev, cells), F32),
                 pltpu.VMEM((nv * lev, lev), F32),
                 dma((7,)),
+                pltpu.VMEM((20, *state[1:]), F32), pltpu.VMEM(state, F32),
                 pltpu.VMEM(state, F32), pltpu.VMEM(state, F32), pltpu.VMEM(state, F32),
-                pltpu.VMEM(state, F32), pltpu.VMEM(state, F32), pltpu.VMEM(state, F32),
-                pltpu.VMEM(strips, F32), pltpu.VMEM(strips, F32),
+                pltpu.VMEM(state, F32),
+                pltpu.VMEM((4, 48 * rows_dev + 2 * PAD, 128), F32),
+                pltpu.VMEM((4, 48 * rows_dev + 2 * PAD, 128), F32),
                 pltpu.VMEM(strips, F32), pltpu.VMEM(strips, F32),
                 products, pltpu.VMEM((256, 256), jnp.bfloat16),
                 packet, packet, packet, packet, packet,
@@ -618,9 +685,12 @@
                 pltpu.VMEM((n, 4, 8, 128), F32),
                 pltpu.VMEM((4, 8, 128), F32),
                 pltpu.VMEM((2, 2, 4, 8, 128), F32),
-                pltpu.VMEM((rows_dev, 4, 40, 128), F32),
+                pltpu.VMEM((rows_dev, 5, 8, 128), F32),
+                pltpu.VMEM((rows_dev - 2, 5, 8, 128), F32),
+                pltpu.VMEM((rows_dev - 2, 5, 8, 128), F32),
+                pltpu.VMEM((rows_dev, 8, 128), F32),
                 small, small, small, small,
-                dma((9,)), dma((10,)), dma((1,)), dma((1,)),
+                dma((11,)), dma((12,)), dma((1,)), dma((1,)),
                 regular((2,)), regular((2,)), regular((4,)),
             ],
             compiler_params=pltpu.CompilerParams(

time: 14.2 us -> 12.7 us (0.89)
  the two profiles are of different devices: /device:TPU:29 before, /device:TPU:0 now
where the time goes in v2:
time: 12.7 us; the launch traced here: 12.6 us
  Pallas kernels  12 us (94%)
  between operations  0.64 us (5%)
    pallas_call x1, Pallas kernels, shards(): pl.pallas_call(functools.partial(kernel, n, n_lat, cells, rows_dev), out_...  10.8 us
    pallas_call x1, Pallas kernels, shards(): pl.pallas_call(finish, out_shape=(shape((flat, cells), F32), shape((flat,...  1.17 us

profile of v2, /device:TPU:0, one launch (start us, length us, event | category | flops | bytes accessed | tf_op | source)
XLA Modules:
  0.0 12.6 jit_solution(5019813986636100243)
XLA Ops:
  0.6 10.8 %shard_map.94 = (f32[1536,128]{1,0:T(8,128)S(1)}, f32[1536,128]{1,0:T(8,128)S(1)}, f32[4,4,128]{2,1,0:T(4,128)S(1)}) custom-call(s32[4]{0:T(128)} %len_hbm.1, f32[1536,128]{1,0:T(8,128)} %bitcast.7, f32[128,128]{1,0:T(8,128)} %bitcast.9, s32[4,128]{1,0:T(4,128)} %own_hbm.1, f32[1536,128]{1,0:T(8,128)} %bitcast.8, f32[128,128]{1,0:T(8,128)} %bitcast.10, ...), custom_call_target="tpu_custom_call" | custom-call | tf_op jit(solution)/shard_map/pallas_call | solution.py:659
  11.4 1.2 %shard_map.95 = (f32[1536,128]{1,0:T(8,128)}, f32[1536,128]{1,0:T(8,128)}, f32[4,4,128]{2,1,0:T(4,128)}) custom-call(f32[1536,128]{1,0:T(8,128)S(1)} %get-tuple-element.9.zo, f32[1536,128]{1,0:T(8,128)S(1)} %get-tuple-element.10.mo, f32[4,4,128]{2,1,0:T(4,128)S(1)} %get-tuple-element.11.co), custom_call_target="tpu_custom_call" | custom-call | tf_op jit(solution)/shard_map/pallas_call | solution.py:713

commit v3 on v2

--- a/solution.py
+++ b/solution.py
@@ -13,6 +13,8 @@
 STEP = 32
 UNSCALE = 10.0**-SUB
 MESH = pl.DeviceIdType.MESH
+LEFT, RIGHT, MERID, TAIL, HEAD = range(5)
+NEAR, PART, WINDOW = 0, 1, 5
 F32 = jnp.float32
 
 
@@ -80,8 +82,8 @@
                 dst[w, pl.ds(PAD + at, step), :] = new[w] * UNSCALE if t == SUB - 1 else new[w]
 
 
-def load_state(state, field, courant, cells, rows_dev):
-    for r in range(rows_dev):
+def load_state(state, field, courant, cells, rows_dev, rows):
+    for r in rows:
         for w in range(3):
             at = w * rows_dev + r
             block = field[pl.ds(at, 128, stride=3 * rows_dev), :]
@@ -90,13 +92,6 @@
         state[12 + r, pl.ds(PAD, cells), :] = jnp.concatenate([5.0 * levels] * 4, axis=0).T
 
 
-def store_state(out, state, cells, rows_dev):
-    for r in range(rows_dev):
-        for w in range(3):
-            at = w * rows_dev + r
-            out[pl.ds(at, 128, stride=3 * rows_dev), :] = state[w * 4 + r, pl.ds(PAD, cells), :].T
-
-
 def pack_ends(first, last, state, cells, rows_dev):
     for r in range(rows_dev):
         for ch in range(4):
@@ -108,14 +103,14 @@
 def kernel(
     n, n_lat, cells, rows_dev,
     len_hbm, z_hbm, zc_hbm, own_hbm, m_hbm, mc_hbm, mix_hbm,
-    zo, mo, co_ref,
-    len_ref, z_ref, zc_ref, own_ref, m_ref, mc_ref, mix_ref, in_sems,
-    zs, zs1, zs2, ms, ms1, ms2, fh, fh1, zh, zh1, products, weights,
+    zs2, ms2, co_ref,
+    len_ref, z_ref, zc_ref, own_ref, m_ref, mc_ref, mix_ref,
+    zs, zs1, ms, ms1, fh, fh1, zh, zh1, products, weights,
     z_first, z_last, z_tail, m_first, m_last,
     from_left, from_right, heads, tails_in, tail_zero, m_halo,
     z_window, w_left, w_right, seam_owner,
     c_left, c_right, c_from_left, c_from_right,
-    sends, recvs, tail_recvs, head_sends,
+    sends, recvs,
     hello_side, hello_merid, hello_far,
 ):
     me = lax.axis_index("lon")
@@ -126,13 +121,13 @@
     mid = n // 2
     last = n - 1
     start = me * cells
+    halves = ((z_hbm.at[:, 1], z_ref.at[:, 1]), (z_hbm.at[:, 0], z_ref.at[:, 0]))
     loads = [
-        pltpu.make_async_copy(src, dst, in_sems.at[i])
-        for i, (src, dst) in enumerate(
-            (
-                (z_hbm, z_ref), (zc_hbm, zc_ref), (len_hbm, len_ref), (m_hbm, m_ref),
-                (mc_hbm, mc_ref), (mix_hbm, mix_ref), (own_hbm, own_ref),
-            )
+        pltpu.make_async_copy(src, dst, sends.at[sem])
+        for src, dst, sem in (
+            (*halves[0], LEFT), (zc_hbm, zc_ref, RIGHT), (len_hbm, len_ref, TAIL),
+            (*halves[1], 5), (m_hbm, m_ref, MERID), (mc_hbm, mc_ref, HEAD),
+            (mix_hbm, mix_ref, 6), (own_hbm, own_ref, 7),
         )
     ]
     for load in loads:
@@ -215,18 +210,6 @@
 
     for load in loads[:3]:
         load.wait()
-    load_state(zs, z_ref, zc_ref, cells, rows_dev)
-    pack_ends(z_first, z_last, zs, cells, rows_dev)
-    lengths = [len_ref[r] for r in range(rows_dev)]
-    index8 = lax.broadcasted_iota(jnp.int32, (8, 128), 0)
-    for r in range(rows_dev):
-        at = jnp.clip(lengths[r] - 4 - start, -4, cells)
-        cell = lengths[r] - 4 - start + index8
-        own = (cell >= 0) & (cell < cells)
-        for ch in range(4):
-            value = zs[ch * 4 + r, pl.ds(PAD + at, 8), :]
-            z_tail[r // 2, ch, pl.ds((r % 2) * 4, 4), :] = jnp.where(own, value, 0.0)[:4]
-
     def copy(src, dst, send, recv, lon_to, lat_to):
         return pltpu.make_async_remote_copy(
             src_ref=src, dst_ref=dst, send_sem=send, recv_sem=recv,
@@ -234,23 +217,42 @@
         )
 
     def head_copy(j):
-        return copy(z_first.at[1], heads.at[1], head_sends.at[0], recvs.at[4], j, lat)
-
-    head_mid = copy(z_first.at[0], heads.at[0], sends.at[5], recvs.at[5], mid, lat)
-    head_last = copy(z_first.at[0], heads.at[0], sends.at[8], recvs.at[9], last, lat)
-    tail_mid = copy(z_tail.at[0], tail_zero, sends.at[5], recvs.at[6], 0, lat)
-    tail_last = copy(z_last.at[0], from_left.at[0], sends.at[8], recvs.at[9], 0, lat)
+        return copy(z_first.at[1], heads.at[1], sends.at[HEAD], recvs.at[HEAD], j, lat)
+
+    head_mid = copy(z_first.at[0], heads.at[0], sends.at[HEAD], recvs.at[HEAD], mid, lat)
+    head_last = copy(z_first.at[0], heads.at[0], sends.at[HEAD], recvs.at[HEAD], last, lat)
+    tail_mid = copy(z_tail.at[0], tail_zero, sends.at[TAIL], recvs.at[TAIL], 0, lat)
+    tail_last = copy(z_last.at[0], from_left.at[0], sends.at[TAIL], recvs.at[TAIL], 0, lat)
 
     def tail_copy(j):
-        return copy(z_tail.at[1], tails_in.at[j], sends.at[4], tail_recvs.at[0], 0, lat)
-
-    to_right = copy(z_last, from_left, sends.at[0], recvs.at[0], right, lat)
-    to_left = copy(z_first, from_right, sends.at[1], recvs.at[1], left, lat)
+        return copy(z_tail.at[1], tails_in.at[j], sends.at[TAIL], recvs.at[TAIL], 0, lat)
+
+    to_right = copy(z_last, from_left, sends.at[RIGHT], recvs.at[NEAR], right, lat)
+    to_left = copy(z_first, from_right, sends.at[LEFT], recvs.at[NEAR], left, lat)
+
+    lengths = [len_ref[r] for r in range(rows_dev)]
+    index8 = lax.broadcasted_iota(jnp.int32, (8, 128), 0)
+
+    def load_rows(rows):
+        load_state(zs, z_ref.reshape(m_ref.shape), zc_ref, cells, rows_dev, rows)
+        for r in rows:
+            at = jnp.clip(lengths[r] - 4 - start, -4, cells)
+            cell = lengths[r] - 4 - start + index8
+            own = (cell >= 0) & (cell < cells)
+            for ch in range(4):
+                value = zs[ch * 4 + r, pl.ds(PAD + at, 8), :]
+                z_tail[r // 2, ch, pl.ds((r % 2) * 4, 4), :] = jnp.where(own, value, 0.0)[:4]
+
+    load_rows(range(2, rows_dev))
 
     @pl.when(is_far)
     def _():
         tail_copy(me).start()
 
+    loads[3].wait()
+    load_rows(range(2))
+    pack_ends(z_first, z_last, zs, cells, rows_dev)
+
     @pl.when(me == mid)
     def _():
         tail_mid.start()
@@ -267,15 +269,15 @@
     def _():
         to_right.start()
 
-    for load in loads[3:]:
+    for load in loads[4:6]:
         load.wait()
-    load_state(ms, m_ref, mc_ref, cells, rows_dev)
+    load_state(ms, m_ref, mc_ref, cells, rows_dev, range(rows_dev))
     pack_ends(m_first, m_last, ms, cells, rows_dev)
     to_south = copy(
-        m_first, m_halo.at[south_slot], sends.at[2], recvs.at[2 + south_slot], south_lon, south_lat
+        m_first, m_halo.at[south_slot], sends.at[MERID], recvs.at[MERID], south_lon, south_lat
     )
     to_north = copy(
-        m_last, m_halo.at[north_slot], sends.at[3], recvs.at[2 + north_slot], north_lon, north_lat
+        m_last, m_halo.at[north_slot], sends.at[MERID], recvs.at[MERID], north_lon, north_lat
     )
 
     def over_poles(some):
@@ -293,6 +295,8 @@
 
     over_poles((me >= mid) & (me < mid + 2))
 
+    for load in loads[6:]:
+        load.wait()
     tiled = jnp.concatenate([mix_ref[...]] * 4, axis=1)
     index_of = lambda axis: lax.broadcasted_iota(jnp.int32, (128, 128), axis)
     block_of = lambda axis: index_of(axis) // 32
@@ -338,30 +342,34 @@
                     head_last.start()
 
     ends = [jnp.clip(lengths[r] - start, 0, cells) for r in range(rows_dev)]
-    for src, dst in ((zs, zs1), (zs1, zs2), (zs2, zs1)):
+    for src, dst in ((zs, zs1), (zs1, zs2)):
         advance(src, dst, zs, products, weights, cells, rows_dev, None)
+    @pl.when(jnp.logical_not(at_north))
+    def _():
+        pl.semaphore_wait(hello_merid.at[1], 1)
+        to_north.start()
+
+    def ready_poles(some):
+        @pl.when(at_south & some)
+        def _():
+            pl.semaphore_wait(hello_merid.at[0], 1)
+
+        @pl.when(at_north & some)
+        def _():
+            pl.semaphore_wait(hello_merid.at[1], 1)
+
+    ready_poles((me > 1) & (me < mid))
+    over_poles((me > 1) & ((me < mid) | (me >= mid + 2)))
+
+    advance(zs2, zs1, zs, products, weights, cells, rows_dev, None)
     advance(zs1, zs2, zs, products, weights, cells, rows_dev, ends, final=True)
     always = me >= 0
     serve(0, always)
     serve(1, always)
     serve(2, lat > 0)
 
-    @pl.when(jnp.logical_not(at_north))
-    def _():
-        pl.semaphore_wait(hello_merid.at[1], 1)
-        to_north.start()
-
-    def ready_poles(some):
-        @pl.when(at_south & some)
-        def _():
-            pl.semaphore_wait(hello_merid.at[0], 1)
-
-        @pl.when(at_north & some)
-        def _():
-            pl.semaphore_wait(hello_merid.at[1], 1)
-
-    ready_poles((me > 1) & (me < mid))
-    over_poles((me > 1) & ((me < mid) | (me >= mid + 2)))
+    ready_poles((me <= 1) & (lat > 0))
+    over_poles((me <= 1) & (lat > 0))
 
     for r in range(rows_dev):
         owners = (own_ref[pl.ds(r, 1), :] + 1).astype(F32)
@@ -373,8 +381,8 @@
             value = zs[ch * 4 + r, pl.ds(PAD + at, 8), :]
             z_window[r, ch, :, :] = jnp.where((cell >= 0) & (cell < cells), value, 0.0)
     moving = z_window.at[pl.ds(2, rows_dev - 2)]
-    window_left = copy(moving, w_right, sends.at[9], recvs.at[10], left, lat)
-    window_right = copy(moving, w_left, sends.at[10], recvs.at[11], right, lat)
+    window_left = copy(moving, w_right, sends.at[LEFT], recvs.at[WINDOW], left, lat)
+    window_right = copy(moving, w_left, sends.at[RIGHT], recvs.at[WINDOW], right, lat)
 
     @pl.when(has_left)
     def _():
@@ -388,12 +396,6 @@
         advance(src, dst, ms, products, weights, cells, rows_dev, None)
     serve(2, at_south)
     serve(3, lat > 0)
-    for src, dst in ((ms2, ms1), (ms1, ms2)):
-        advance(src, dst, ms, products, weights, cells, rows_dev, None, final=dst is ms2)
-    serve(3, at_south)
-    ready_poles(me <= 1)
-    over_poles(me <= 1)
-
     def fill_left():
         for r in range(rows_dev):
             take = pl.ds((r % 2) * 4, 4)
@@ -430,18 +432,29 @@
         half = both.shape[1] // 2
         return both[:, :half] + both[:, half:]
 
-    part_left = copy(c_left, c_from_right, sends.at[6], recvs.at[7], left, lat)
-    part_right = copy(c_right, c_from_left, sends.at[7], recvs.at[8], right, lat)
-
-    @pl.when(has_right)
-    def _():
-        to_right.wait_send()
-        to_left.wait_recv()
-
-    @pl.when(has_left)
-    def _():
-        to_left.wait_send()
-        to_right.wait_recv()
+    part_left = copy(c_left, c_from_right, sends.at[LEFT], recvs.at[PART], left, lat)
+    part_right = copy(c_right, c_from_left, sends.at[RIGHT], recvs.at[PART], right, lat)
+
+    def transfers(count, sem):
+        lines = products.at[pl.ds(0, count)]
+        return copy(lines, lines, sends.at[sem], recvs.at[sem], partner, lat)
+
+    both = has_left & has_right
+    one_side = jnp.logical_not(both)
+    ends_here = (me == mid) | (me == last)
+    plain_far = is_far & jnp.logical_not(ends_here)
+    all_tails = (n - wrap_from + 2) * 32
+
+    def beside(count, sem):
+        @pl.when(both)
+        def _():
+            transfers(2 * count, sem).wait_recv()
+
+        @pl.when(one_side)
+        def _():
+            transfers(count, sem).wait_recv()
+
+    beside(64, NEAR)
 
     @pl.when(has_left)
     def _():
@@ -480,44 +493,28 @@
     def _():
         part_right.start()
 
-    copy(m_first, m_halo.at[0], sends.at[2], recvs.at[2], south_lon, south_lat).wait()
-    copy(m_last, m_halo.at[1], sends.at[3], recvs.at[3], north_lon, north_lat).wait()
-
-    @pl.when(is_far)
-    def _():
-        tail_copy(me).wait_send()
-        head_copy(me).wait_recv()
-
-    @pl.when(me == mid)
-    def _():
-        tail_mid.wait_send()
-        head_mid.wait_recv()
-
-    @pl.when(me == last)
-    def _():
-        tail_last.wait_send()
-        head_last.wait_recv()
-
-    @pl.when(has_left)
-    def _():
-        window_left.wait_send()
-        window_right.wait_recv()
-
-    @pl.when(has_right)
-    def _():
-        window_right.wait_send()
-        window_left.wait_recv()
+    ready_poles((me <= 1) & at_south)
+    over_poles((me <= 1) & at_south)
+
+    serve(3, at_south)
+
+    for src, dst in ((ms2, ms1), (ms1, ms2)):
+        advance(src, dst, ms, products, weights, cells, rows_dev, None, final=dst is ms2)
+    transfers(128, MERID).wait_recv()
+
+    @pl.when(plain_far)
+    def _():
+        transfers(32, HEAD).wait_recv()
+
+    @pl.when(ends_here)
+    def _():
+        transfers(64, HEAD).wait_recv()
+
+    beside((rows_dev - 2) * 40, WINDOW)
 
     @pl.when(is_hub)
     def _():
-        every = tails_in.at[pl.ds(wrap_from, n - wrap_from)]
-        all_far = copy(every, every, head_sends.at[0], tail_recvs.at[0], last, lat)
-        all_far.wait_send()
-        all_far.wait_recv()
-        head_mid.wait_send()
-        tail_mid.wait_recv()
-        head_last.wait_send()
-        tail_last.wait_recv()
+        transfers(all_tails, TAIL).wait_recv()
 
     @pl.when(is_hub)
     def _():
@@ -580,7 +577,6 @@
             at, base = w * 4 + r, merid + r * 32
             ms2[at, pl.ds(PAD, 4), :] = fh[w, pl.ds(base + 4, 4), :]
             ms2[at, pl.ds(PAD + cells - 4, 4), :] = fh[w, pl.ds(base + 20, 4), :]
-    store_state(mo, ms2, cells, rows_dev)
 
     @pl.when(is_hub)
     def _():
@@ -602,7 +598,6 @@
                         inside, fh[w, pl.ds(take, 8), :], old
                     )
 
-    store_state(zo, zs2, cells, rows_dev)
     for r in range(rows_dev):
         delta = (wanted(r) - seam_before[r]) * scale
         owner = seam_owner[r, pl.ds(0, 4), :]
@@ -612,30 +607,48 @@
                 jnp.where(mine, delta, 0.0), axis=0, keepdims=True
             )
 
+    beside(8, PART)
+
     @pl.when(has_left)
     def _():
-        part_left.wait_send()
-        part_right.wait_recv()
         for r in range(rows_dev):
             co_ref[0, pl.ds(r, 1), :] += c_from_left[pl.ds(r, 1), :]
 
     @pl.when(has_right)
     def _():
-        part_right.wait_send()
-        part_left.wait_recv()
         for r in range(rows_dev):
             co_ref[GLON_DEV - 1, pl.ds(r, 1), :] += c_from_right[pl.ds(r, 1), :]
 
-
-def finish(zo, mo, co, zo_hbm, mo_hbm, co_hbm, sems):
-    copies = [
-        pltpu.make_async_copy(src, dst, sems.at[i])
-        for i, (src, dst) in enumerate(((zo, zo_hbm), (mo, mo_hbm), (co, co_hbm)))
-    ]
-    for out in copies:
-        out.start()
-    for out in copies:
-        out.wait()
+    sideways = 64 + (rows_dev - 2) * 40 + 8
+    transfers(128, MERID).wait_send()
+    for flag, count, sem in (
+        (has_left, sideways, LEFT),
+        (has_right, sideways, RIGHT),
+        (plain_far, 32, TAIL),
+        (ends_here, 64, TAIL),
+        (is_hub, all_tails, HEAD),
+    ):
+
+        @pl.when(flag)
+        def _():
+            transfers(count, sem).wait_send()
+
+
+def finish(cells, rows_dev, zs, ms, co, zo_hbm, mo_hbm, co_hbm, zo, mo, sems):
+    copies = [pltpu.make_async_copy(co, co_hbm, sems.at[6])]
+    copies[0].start()
+    for i, (state, staged, out) in enumerate(((ms, mo, mo_hbm), (zs, zo, zo_hbm))):
+        for w in range(3):
+            rows = staged.at[w].reshape(128 * rows_dev, cells)
+            for r in range(rows_dev):
+                block = state[w * 4 + r, pl.ds(PAD, cells), :]
+                rows[pl.ds(r, 128, stride=rows_dev), :] = block.T
+            copies.append(
+                pltpu.make_async_copy(staged.at[w], out.at[:, w], sems.at[3 * i + w])
+            )
+            copies[-1].start()
+    for done in copies:
+        done.wait()
 
 
 def solution(mesh):
@@ -659,23 +672,21 @@
         held = pl.pallas_call(
             functools.partial(kernel, n, n_lat, cells, rows_dev),
             out_shape=(
-                shape((flat, cells), F32), shape((flat, cells), F32),
+                shape(state, F32), shape(state, F32),
                 shape((GLON_DEV, rows_dev, nv * lev), F32),
             ),
             in_specs=[hbm] * 7,
             out_specs=(vmem,) * 3,
             scratch_shapes=[
                 pltpu.SMEM((rows_dev,), jnp.int32),
-                pltpu.VMEM((flat, cells), F32),
+                pltpu.VMEM((nv * lev * wid, 2, rows_dev // 2, cells), F32),
                 pltpu.VMEM((lev * rows_dev, cells), F32),
                 pltpu.VMEM((rows_dev, cells), jnp.int32),
                 pltpu.VMEM((flat, cells), F32),
                 pltpu.VMEM((lev * rows_dev, cells), F32),
                 pltpu.VMEM((nv * lev, lev), F32),
-                dma((7,)),
                 pltpu.VMEM((20, *state[1:]), F32), pltpu.VMEM(state, F32),
-                pltpu.VMEM(state, F32), pltpu.VMEM(state, F32), pltpu.VMEM(state, F32),
-                pltpu.VMEM(state, F32),
+                pltpu.VMEM(state, F32), pltpu.VMEM(state, F32),
                 pltpu.VMEM((4, 48 * rows_dev + 2 * PAD, 128), F32),
                 pltpu.VMEM((4, 48 * rows_dev + 2 * PAD, 128), F32),
                 pltpu.VMEM(strips, F32), pltpu.VMEM(strips, F32),
@@ -690,7 +701,7 @@
                 pltpu.VMEM((rows_dev - 2, 5, 8, 128), F32),
                 pltpu.VMEM((rows_dev, 8, 128), F32),
                 small, small, small, small,
-                dma((11,)), dma((12,)), dma((1,)), dma((1,)),
+                dma((8,)), dma((6,)),
                 regular((2,)), regular((2,)), regular((4,)),
             ],
             compiler_params=pltpu.CompilerParams(
@@ -701,7 +712,7 @@
                 pltpu.with_memory_space_constraint(value, pltpu.HBM)
                 for value in (
                     zonal_length,
-                    zonal_state.reshape(flat, cells),
+                    zonal_state.reshape(nv * lev * wid, 2, rows_dev // 2, cells),
                     zonal_courant.reshape(lev * rows_dev, cells),
                     zonal_owner,
                     merid_state.reshape(flat, cells),
@@ -711,14 +722,19 @@
             )
         )
         zo, mo, co = pl.pallas_call(
-            finish,
+            functools.partial(finish, cells, rows_dev),
             out_shape=(
-                shape((flat, cells), F32), shape((flat, cells), F32),
+                shape((nv * lev, wid, rows_dev, cells), F32),
+                shape((nv * lev, wid, rows_dev, cells), F32),
                 shape((GLON_DEV, rows_dev, nv * lev), F32),
             ),
             in_specs=[vmem] * 3,
             out_specs=(hbm,) * 3,
-            scratch_shapes=[dma((3,))],
+            scratch_shapes=[
+                pltpu.VMEM((wid, nv * lev, rows_dev, cells), F32),
+                pltpu.VMEM((wid, nv * lev, rows_dev, cells), F32),
+                dma((7,)),
+            ],
             compiler_params=pltpu.CompilerParams(vmem_limit_bytes=40 * 1024 * 1024),
         )(*held)
         return zo.reshape(zonal_state.shape), mo.reshape(merid_state.shape), co

time: 12.7 us -> 12.2 us (0.961)
  Pallas kernels: 12 us -> 11.4 us
    pallas_call x1, Pallas kernels: 10.8 us -> 10 us  [shards(): pl.pallas_call(functools.partial(kernel, n, n_lat, cells, rows_dev), out_...]
    pallas_call x1, Pallas kernels: 1.17 us -> 1.33 us  [shards(): pl.pallas_call(functools.partial(finish, cells, rows_dev), out_shape=(sha...]
where the time goes in v3:
time: 12.2 us; the launch traced here: 12 us
  Pallas kernels  11.4 us (93%)
  between operations  0.64 us (5%)
    pallas_call x1, Pallas kernels, shards(): pl.pallas_call(functools.partial(kernel, n, n_lat, cells, rows_dev), out_...  10 us
    pallas_call x1, Pallas kernels, shards(): pl.pallas_call(functools.partial(finish, cells, rows_dev), out_shape=(sha...  1.33 us

profile of v3, /device:TPU:0, one launch (start us, length us, event | category | flops | bytes accessed | tf_op | source)
XLA Modules:
  0.0 12.0 jit_solution(4008598665196439178)
XLA Ops:
  0.6 10.0 %shard_map.94 = (f32[16,144,128]{2,1,0:T(8,128)S(1)}, f32[16,144,128]{2,1,0:T(8,128)S(1)}, f32[4,4,128]{2,1,0:T(4,128)S(1)}) custom-call(s32[4]{0:T(128)} %len_hbm.1, f32[384,2,2,128]{3,2,1,0:T(2,128)} %bitcast.7, f32[128,128]{1,0:T(8,128)} %bitcast.9, s32[4,128]{1,0:T(4,128)} %own_hbm.1, f32[1536,128]{1,0:T(8,128)} %bitcast.8, f32[128,128]{1,0:T(8,128)} %bitcast.10, ...), custom_call_target="tpu_custom_call" | custom-call | tf_op jit(solution)/shard_map/pallas_call | solution.py:672
  10.7 1.3 %shard_map.95 = (f32[128,3,4,128]{3,2,1,0:T(4,128)}, f32[128,3,4,128]{3,2,1,0:T(4,128)}, f32[4,4,128]{2,1,0:T(4,128)}) custom-call(f32[16,144,128]{2,1,0:T(8,128)S(1)} %get-tuple-element.9.zs, f32[16,144,128]{2,1,0:T(8,128)S(1)} %get-tuple-element.10.ms, f32[4,4,128]{2,1,0:T(4,128)S(1)} %get-tuple-element.11.co), custom_call_target="tpu_custom_call" | custom-call | tf_op jit(solution)/shard_map/pallas_call | solution.py:724

commit v4 on v3

--- a/solution.py
+++ b/solution.py
@@ -66,8 +66,7 @@
                 dst[w * 4 + r, pl.ds(PAD + at, step), :] = value
 
 
-def advance_strips(first, second, products, weights, rows):
-    step = STEP
+def advance_strips(first, second, products, weights, rows, step):
     for t in range(SUB):
         src, dst = (first, second) if t % 2 == 0 else (second, first)
         mix_into(products, 0, [src[w, pl.ds(PAD, rows), :] for w in range(3)], weights)
@@ -208,7 +207,7 @@
     def _():
         hello(hello_merid.at[north_slot], north_lon, north_lat)
 
-    for load in loads[:3]:
+    for load in loads[:2]:
         load.wait()
     def copy(src, dst, send, recv, lon_to, lat_to):
         return pltpu.make_async_remote_copy(
@@ -221,45 +220,53 @@
 
     head_mid = copy(z_first.at[0], heads.at[0], sends.at[HEAD], recvs.at[HEAD], mid, lat)
     head_last = copy(z_first.at[0], heads.at[0], sends.at[HEAD], recvs.at[HEAD], last, lat)
-    tail_mid = copy(z_tail.at[0], tail_zero, sends.at[TAIL], recvs.at[TAIL], 0, lat)
-    tail_last = copy(z_last.at[0], from_left.at[0], sends.at[TAIL], recvs.at[TAIL], 0, lat)
+    tail_mid = copy(z_tail.at[1], tail_zero, sends.at[TAIL], recvs.at[TAIL], 0, lat)
+    tail_last = copy(z_tail.at[2], from_left.at[0], sends.at[TAIL], recvs.at[TAIL], 0, lat)
 
     def tail_copy(j):
-        return copy(z_tail.at[1], tails_in.at[j], sends.at[TAIL], recvs.at[TAIL], 0, lat)
+        return copy(z_tail.at[0], tails_in.at[j], sends.at[TAIL], recvs.at[TAIL], 0, lat)
 
     to_right = copy(z_last, from_left, sends.at[RIGHT], recvs.at[NEAR], right, lat)
     to_left = copy(z_first, from_right, sends.at[LEFT], recvs.at[NEAR], left, lat)
 
-    lengths = [len_ref[r] for r in range(rows_dev)]
     index8 = lax.broadcasted_iota(jnp.int32, (8, 128), 0)
 
     def load_rows(rows):
         load_state(zs, z_ref.reshape(m_ref.shape), zc_ref, cells, rows_dev, rows)
+
+    def pack_tails(rows, packet):
         for r in rows:
             at = jnp.clip(lengths[r] - 4 - start, -4, cells)
             cell = lengths[r] - 4 - start + index8
             own = (cell >= 0) & (cell < cells)
             for ch in range(4):
                 value = zs[ch * 4 + r, pl.ds(PAD + at, 8), :]
-                z_tail[r // 2, ch, pl.ds((r % 2) * 4, 4), :] = jnp.where(own, value, 0.0)[:4]
+                z_tail[packet, ch, pl.ds((r % 2) * 4, 4), :] = jnp.where(own, value, 0.0)[:4]
 
     load_rows(range(2, rows_dev))
+    loads[2].wait()
+    lengths = [len_ref[r] for r in range(rows_dev)]
+    pack_tails(range(2, rows_dev), 0)
 
     @pl.when(is_far)
     def _():
         tail_copy(me).start()
 
     loads[3].wait()
-    load_rows(range(2))
+    load_rows(range(1, 2))
+    pack_tails(range(1, 2), 2)
+
+    @pl.when(me == last)
+    def _():
+        tail_last.start()
+
+    load_rows(range(1))
+    pack_tails(range(1), 1)
     pack_ends(z_first, z_last, zs, cells, rows_dev)
 
     @pl.when(me == mid)
     def _():
         tail_mid.start()
-
-    @pl.when(me == last)
-    def _():
-        tail_last.start()
 
     @pl.when(left_earlier)
     def _():
@@ -368,8 +375,9 @@
     serve(1, always)
     serve(2, lat > 0)
 
-    ready_poles((me <= 1) & (lat > 0))
-    over_poles((me <= 1) & (lat > 0))
+    first_chip = ((me == 0) & (lat > 0)) | (me == 1)
+    ready_poles(first_chip)
+    over_poles(first_chip)
 
     for r in range(rows_dev):
         owners = (own_ref[pl.ds(r, 1), :] + 1).astype(F32)
@@ -384,18 +392,16 @@
     window_left = copy(moving, w_right, sends.at[LEFT], recvs.at[WINDOW], left, lat)
     window_right = copy(moving, w_left, sends.at[RIGHT], recvs.at[WINDOW], right, lat)
 
-    @pl.when(has_left)
+    far_left, far_right = me > wrap_from, is_far & has_right
+
+    @pl.when(far_left)
     def _():
         window_left.start()
 
-    @pl.when(has_right)
+    @pl.when(far_right)
     def _():
         window_right.start()
 
-    for src, dst in ((ms, ms1), (ms1, ms2)):
-        advance(src, dst, ms, products, weights, cells, rows_dev, None)
-    serve(2, at_south)
-    serve(3, lat > 0)
     def fill_left():
         for r in range(rows_dev):
             take = pl.ds((r % 2) * 4, 4)
@@ -439,22 +445,20 @@
         lines = products.at[pl.ds(0, count)]
         return copy(lines, lines, sends.at[sem], recvs.at[sem], partner, lat)
 
-    both = has_left & has_right
-    one_side = jnp.logical_not(both)
     ends_here = (me == mid) | (me == last)
     plain_far = is_far & jnp.logical_not(ends_here)
     all_tails = (n - wrap_from + 2) * 32
 
-    def beside(count, sem):
-        @pl.when(both)
+    def beside(count, sem, from_left, from_right):
+        @pl.when(from_left & from_right)
         def _():
             transfers(2 * count, sem).wait_recv()
 
-        @pl.when(one_side)
+        @pl.when(jnp.logical_xor(from_left, from_right))
         def _():
             transfers(count, sem).wait_recv()
 
-    beside(64, NEAR)
+    beside(64, NEAR, has_left, has_right)
 
     @pl.when(has_left)
     def _():
@@ -469,7 +473,7 @@
             base = PAD + r * 32
             zh[ch, pl.ds(base, 16), :] = zs[ch * 4 + r, pl.ds(PAD - 4, 16), :]
             zh[ch, pl.ds(base + 16, 16), :] = zs[ch * 4 + r, pl.ds(PAD + cells - 8, 16), :]
-    advance_strips(zh, zh1, products, weights, 32 * rows_dev)
+    advance_strips(zh, zh1, products, weights, 32 * rows_dev, STEP)
     for r in range(rows_dev):
         base = PAD + r * 32
         for w in range(3):
@@ -493,8 +497,12 @@
     def _():
         part_right.start()
 
-    ready_poles((me <= 1) & at_south)
-    over_poles((me <= 1) & at_south)
+    for src, dst in ((ms, ms1), (ms1, ms2)):
+        advance(src, dst, ms, products, weights, cells, rows_dev, None)
+    serve(2, at_south)
+    serve(3, lat > 0)
+    ready_poles(is_hub & at_south)
+    over_poles(is_hub & at_south)
 
     serve(3, at_south)
 
@@ -510,7 +518,7 @@
     def _():
         transfers(64, HEAD).wait_recv()
 
-    beside((rows_dev - 2) * 40, WINDOW)
+    beside((rows_dev - 2) * 40, WINDOW, far_left, far_right)
 
     @pl.when(is_hub)
     def _():
@@ -523,12 +531,12 @@
             for j in range(wrap_from + 1, n):
                 total = total + tails_in[j, ch]
             fh[ch, pl.ds(PAD, 4), :] = tail_zero[ch, pl.ds(0, 4), :]
-            fh[ch, pl.ds(PAD + 16, 4), :] = from_left[0, ch, pl.ds(4, 4), :]
+            fh[ch, pl.ds(PAD + 12, 4), :] = from_left[0, ch, pl.ds(4, 4), :]
             for r in range(2, rows_dev):
                 half = (r % 2) * 4
-                fh[ch, pl.ds(PAD + 16 * r, 4), :] = total[half : half + 4]
+                fh[ch, pl.ds(PAD + 12 * r, 4), :] = total[half : half + 4]
             for r in range(rows_dev):
-                fh[ch, pl.ds(PAD + 16 * r + 4, 12), :] = zs[ch * 4 + r, pl.ds(PAD, 12), :]
+                fh[ch, pl.ds(PAD + 12 * r + 4, 8), :] = zs[ch * 4 + r, pl.ds(PAD, 8), :]
         for r in range(rows_dev):
             seam_owner[r, :, :] = zs[16 + r, pl.ds(PAD, 8), :]
 
@@ -538,51 +546,49 @@
             for ch in range(5):
                 window = z_window[r, ch]
                 if r >= 2:
-                    window = window + w_left[r - 2, ch]
-                    window = window + jnp.where(has_right, w_right[r - 2, ch], 0.0)
+                    window = window + jnp.where(far_left, w_left[r - 2, ch], 0.0)
+                    window = window + jnp.where(far_right, w_right[r - 2, ch], 0.0)
                 if ch == 4:
                     seam_owner[r, pl.ds(0, 4), :] = window[4:8]
                     continue
-                base = PAD + 16 * r
+                base = PAD + 12 * r
                 fh[ch, pl.ds(base, 8), :] = window
                 fh[ch, pl.ds(base + 8, 4), :] = heads[r // 2, ch, pl.ds((r % 2) * 4, 4), :]
-                fh[ch, pl.ds(base + 12, 4), :] = jnp.zeros((4, 128), F32)
-
-    merid = PAD + 16 * rows_dev
+
+    merid = PAD + 12 * rows_dev
     for r in range(rows_dev):
         take = (r % 2) * 4
         for ch in range(4):
             turned = ch if ch == 3 else 2 - ch
             sign = -1.0 if ch == 3 else 1.0
-            base = merid + r * 32
+            base = merid + r * 24
             for j in range(4):
                 plain = m_halo[0, r // 2, ch, pl.ds(take + j, 1), :]
                 pole = sign * m_halo[0, r // 2, turned, pl.ds(take + 3 - j, 1), :]
                 fh[ch, pl.ds(base + j, 1), :] = jnp.where(at_south, pole, plain)
                 plain = m_halo[1, r // 2, ch, pl.ds(take + j, 1), :]
                 pole = sign * m_halo[1, r // 2, turned, pl.ds(take + 3 - j, 1), :]
-                fh[ch, pl.ds(base + 24 + j, 1), :] = jnp.where(at_north, pole, plain)
-            fh[ch, pl.ds(base + 4, 12), :] = ms[ch * 4 + r, pl.ds(PAD, 12), :]
-            fh[ch, pl.ds(base + 16, 8), :] = ms[ch * 4 + r, pl.ds(PAD + cells - 8, 8), :]
-            fh[ch, pl.ds(base + 28, 4), :] = jnp.zeros((4, 128), F32)
+                fh[ch, pl.ds(base + 20 + j, 1), :] = jnp.where(at_north, pole, plain)
+            fh[ch, pl.ds(base + 4, 8), :] = ms[ch * 4 + r, pl.ds(PAD, 8), :]
+            fh[ch, pl.ds(base + 12, 8), :] = ms[ch * 4 + r, pl.ds(PAD + cells - 8, 8), :]
 
     def wanted(r):
-        at = pl.ds(PAD + 16 * r + 4, 4)
+        at = pl.ds(PAD + 12 * r + 4, 4)
         return fh[0, at, :] + fh[1, at, :] + fh[2, at, :]
 
     seam_before = [wanted(r) for r in range(rows_dev)]
-    advance_strips(fh, fh1, products, weights, 48 * rows_dev)
+    advance_strips(fh, fh1, products, weights, 36 * rows_dev, 48)
     for r in range(rows_dev):
         for w in range(3):
-            at, base = w * 4 + r, merid + r * 32
+            at, base = w * 4 + r, merid + r * 24
             ms2[at, pl.ds(PAD, 4), :] = fh[w, pl.ds(base + 4, 4), :]
-            ms2[at, pl.ds(PAD + cells - 4, 4), :] = fh[w, pl.ds(base + 20, 4), :]
+            ms2[at, pl.ds(PAD + cells - 4, 4), :] = fh[w, pl.ds(base + 16, 4), :]
 
     @pl.when(is_hub)
     def _():
         for r in range(rows_dev):
             for w in range(3):
-                zs2[w * 4 + r, pl.ds(PAD, 4), :] = fh[w, pl.ds(PAD + 16 * r + 4, 4), :]
+                zs2[w * 4 + r, pl.ds(PAD, 4), :] = fh[w, pl.ds(PAD + 12 * r + 4, 4), :]
 
     @pl.when(has_left)
     def _():
@@ -590,7 +596,7 @@
             for block in range(0, cells, 8):
                 ahead = block - (lengths[r] - start)
                 inside = (index8 + ahead >= -4) & (index8 + ahead < 0)
-                take = PAD + 16 * r + 8 + jnp.clip(ahead, -12, 0)
+                take = PAD + 12 * r + 8 + jnp.clip(ahead, -12, 0)
                 for w in range(3):
                     at = w * 4 + r
                     old = zs2[at, pl.ds(PAD + block, 8), :]
@@ -607,7 +613,7 @@
                 jnp.where(mine, delta, 0.0), axis=0, keepdims=True
             )
 
-    beside(8, PART)
+    beside(8, PART, has_left, has_right)
 
     @pl.when(has_left)
     def _():
@@ -619,11 +625,13 @@
         for r in range(rows_dev):
             co_ref[GLON_DEV - 1, pl.ds(r, 1), :] += c_from_right[pl.ds(r, 1), :]
 
-    sideways = 64 + (rows_dev - 2) * 40 + 8
+    moved = (rows_dev - 2) * 40
     transfers(128, MERID).wait_send()
     for flag, count, sem in (
-        (has_left, sideways, LEFT),
-        (has_right, sideways, RIGHT),
+        (far_left, 72 + moved, LEFT),
+        (has_left & jnp.logical_not(far_left), 72, LEFT),
+        (far_right, 72 + moved, RIGHT),
+        (has_right & jnp.logical_not(far_right), 72, RIGHT),
         (plain_far, 32, TAIL),
         (ends_here, 64, TAIL),
         (is_hub, all_tails, HEAD),
@@ -687,11 +695,11 @@
                 pltpu.VMEM((nv * lev, lev), F32),
                 pltpu.VMEM((20, *state[1:]), F32), pltpu.VMEM(state, F32),
                 pltpu.VMEM(state, F32), pltpu.VMEM(state, F32),
-                pltpu.VMEM((4, 48 * rows_dev + 2 * PAD, 128), F32),
-                pltpu.VMEM((4, 48 * rows_dev + 2 * PAD, 128), F32),
+                pltpu.VMEM((4, 36 * rows_dev + 2 * PAD, 128), F32),
+                pltpu.VMEM((4, 36 * rows_dev + 2 * PAD, 128), F32),
                 pltpu.VMEM(strips, F32), pltpu.VMEM(strips, F32),
                 products, pltpu.VMEM((256, 256), jnp.bfloat16),
-                packet, packet, packet, packet, packet,
+                packet, packet, pltpu.VMEM((3, 4, 8, 128), F32), packet, packet,
                 packet, packet, packet,
                 pltpu.VMEM((n, 4, 8, 128), F32),
                 pltpu.VMEM((4, 8, 128), F32),

time: 12.2 us -> 12 us (0.984)
  Pallas kernels: 11.4 us -> 11.2 us
    pallas_call x1, Pallas kernels: 10 us -> 9.91 us  [shards(): pl.pallas_call(functools.partial(kernel, n, n_lat, cells, rows_dev), out_...]
where the time goes in v4:
time: 12 us; the launch traced here: 11.9 us
  Pallas kernels  11.2 us (93%)
  between operations  0.64 us (5%)
    pallas_call x1, Pallas kernels, shards(): pl.pallas_call(functools.partial(kernel, n, n_lat, cells, rows_dev), out_...  9.91 us
    pallas_call x1, Pallas kernels, shards(): pl.pallas_call(functools.partial(finish, cells, rows_dev), out_shape=(sha...  1.33 us

profile of v4, /device:TPU:0, one launch (start us, length us, event | category | flops | bytes accessed | tf_op | source)
XLA Modules:
  0.0 11.9 jit_solution(12926565738717302226)
XLA Ops:
  0.6 9.9 %shard_map.94 = (f32[16,144,128]{2,1,0:T(8,128)S(1)}, f32[16,144,128]{2,1,0:T(8,128)S(1)}, f32[4,4,128]{2,1,0:T(4,128)S(1)}) custom-call(s32[4]{0:T(128)} %len_hbm.1, f32[384,2,2,128]{3,2,1,0:T(2,128)} %bitcast.7, f32[128,128]{1,0:T(8,128)} %bitcast.9, s32[4,128]{1,0:T(4,128)} %own_hbm.1, f32[1536,128]{1,0:T(8,128)} %bitcast.8, f32[128,128]{1,0:T(8,128)} %bitcast.10, ...), custom_call_target="tpu_custom_call" | custom-call | tf_op jit(solution)/shard_map/pallas_call | solution.py:680
  10.6 1.3 %shard_map.95 = (f32[128,3,4,128]{3,2,1,0:T(4,128)}, f32[128,3,4,128]{3,2,1,0:T(4,128)}, f32[4,4,128]{2,1,0:T(4,128)}) custom-call(f32[16,144,128]{2,1,0:T(8,128)S(1)} %get-tuple-element.9.zs, f32[16,144,128]{2,1,0:T(8,128)S(1)} %get-tuple-element.10.ms, f32[4,4,128]{2,1,0:T(4,128)S(1)} %get-tuple-element.11.co), custom_call_target="tpu_custom_call" | custom-call | tf_op jit(solution)/shard_map/pallas_call | solution.py:732

commit v5 on v4

--- a/solution.py
+++ b/solution.py
@@ -66,19 +66,23 @@
                 dst[w * 4 + r, pl.ds(PAD + at, step), :] = value
 
 
+def strips_substep(src, dst, fives, products, weights, rows, step, final):
+    mix_into(products, 0, [src[w, pl.ds(PAD, rows), :] for w in range(3)], weights)
+    for at in range(0, rows, step):
+        now = [src[w, pl.ds(PAD + at, step), :] for w in range(3)]
+        ahead = [src[w, pl.ds(PAD + at + 1, step), :] for w in range(3)]
+        behind = [src[w, pl.ds(PAD + at - 1, step), :] for w in range(3)]
+        five = fives[3, pl.ds(PAD + at, step), :]
+        product = [products[pl.ds(w * rows + at, step), :] for w in range(3)]
+        new = updated(now, ahead, behind, five, product)
+        for w in range(3):
+            dst[w, pl.ds(PAD + at, step), :] = new[w] * UNSCALE if final else new[w]
+
+
 def advance_strips(first, second, products, weights, rows, step):
     for t in range(SUB):
         src, dst = (first, second) if t % 2 == 0 else (second, first)
-        mix_into(products, 0, [src[w, pl.ds(PAD, rows), :] for w in range(3)], weights)
-        for at in range(0, rows, step):
-            now = [src[w, pl.ds(PAD + at, step), :] for w in range(3)]
-            ahead = [src[w, pl.ds(PAD + at + 1, step), :] for w in range(3)]
-            behind = [src[w, pl.ds(PAD + at - 1, step), :] for w in range(3)]
-            five = first[3, pl.ds(PAD + at, step), :]
-            product = [products[pl.ds(w * rows + at, step), :] for w in range(3)]
-            new = updated(now, ahead, behind, five, product)
-            for w in range(3):
-                dst[w, pl.ds(PAD + at, step), :] = new[w] * UNSCALE if t == SUB - 1 else new[w]
+        strips_substep(src, dst, first, products, weights, rows, step, t == SUB - 1)
 
 
 def load_state(state, field, courant, cells, rows_dev, rows):
@@ -102,12 +106,12 @@
 def kernel(
     n, n_lat, cells, rows_dev,
     len_hbm, z_hbm, zc_hbm, own_hbm, m_hbm, mc_hbm, mix_hbm,
-    zs2, ms2, co_ref,
+    zs2, ms2, co_ref, fz, seam_owner, seam_room, weights,
     len_ref, z_ref, zc_ref, own_ref, m_ref, mc_ref, mix_ref,
-    zs, zs1, ms, ms1, fh, fh1, zh, zh1, products, weights,
+    zs, zs1, ms, ms1, fh, fh1, zh, zh1, products,
     z_first, z_last, z_tail, m_first, m_last,
     from_left, from_right, heads, tails_in, tail_zero, m_halo,
-    z_window, w_left, w_right, seam_owner,
+    z_window, w_left, w_right,
     c_left, c_right, c_from_left, c_from_right,
     sends, recvs,
     hello_side, hello_merid, hello_far,
@@ -318,7 +322,7 @@
     for slot in range(16):
         zs[slot, pl.ds(0, PAD), :] = zeros
         zs[slot, pl.ds(PAD + cells, PAD), :] = zeros
-    for buf in (zh, zh1, fh, fh1):
+    for buf in (zh, zh1, fh, fh1, fz):
         for ch in range(3):
             buf[ch, pl.ds(0, PAD), :] = zeros
             buf[ch, pl.ds(buf.shape[1] - PAD, PAD), :] = zeros
@@ -401,6 +405,16 @@
     @pl.when(far_right)
     def _():
         window_right.start()
+
+    first_partials = lax.rem(me, 4) == 2
+
+    def merid_begin(some):
+        @pl.when(some)
+        def _():
+            for src, dst in ((ms, ms1), (ms1, ms2)):
+                advance(src, dst, ms, products, weights, cells, rows_dev, None)
+
+    merid_begin(jnp.logical_not(first_partials))
 
     def fill_left():
         for r in range(rows_dev):
@@ -470,14 +484,14 @@
 
     for r in range(rows_dev):
         for ch in range(4):
-            base = PAD + r * 32
-            zh[ch, pl.ds(base, 16), :] = zs[ch * 4 + r, pl.ds(PAD - 4, 16), :]
-            zh[ch, pl.ds(base + 16, 16), :] = zs[ch * 4 + r, pl.ds(PAD + cells - 8, 16), :]
-    advance_strips(zh, zh1, products, weights, 32 * rows_dev, STEP)
-    for r in range(rows_dev):
-        base = PAD + r * 32
+            base = PAD + r * 24
+            zh[ch, pl.ds(base, 12), :] = zs[ch * 4 + r, pl.ds(PAD - 4, 12), :]
+            zh[ch, pl.ds(base + 12, 12), :] = zs[ch * 4 + r, pl.ds(PAD + cells - 8, 12), :]
+    advance_strips(zh, zh1, products, weights, 24 * rows_dev, 48)
+    for r in range(rows_dev):
+        base = PAD + r * 24
         for w in range(3):
-            for cell, take in ((0, base + 4), (cells - 4, base + 20)):
+            for cell, take in ((0, base + 4), (cells - 4, base + 16)):
                 old = zs2[w * 4 + r, pl.ds(PAD + cell, 4), :]
                 zs2[w * 4 + r, pl.ds(PAD + cell, 4), :] = jnp.where(
                     index4 + cell < ends[r], zh[w, pl.ds(take, 4), :], old
@@ -497,8 +511,7 @@
     def _():
         part_right.start()
 
-    for src, dst in ((ms, ms1), (ms1, ms2)):
-        advance(src, dst, ms, products, weights, cells, rows_dev, None)
+    merid_begin(first_partials)
     serve(2, at_south)
     serve(3, lat > 0)
     ready_poles(is_hub & at_south)
@@ -510,58 +523,12 @@
         advance(src, dst, ms, products, weights, cells, rows_dev, None, final=dst is ms2)
     transfers(128, MERID).wait_recv()
 
-    @pl.when(plain_far)
-    def _():
-        transfers(32, HEAD).wait_recv()
-
-    @pl.when(ends_here)
-    def _():
-        transfers(64, HEAD).wait_recv()
-
-    beside((rows_dev - 2) * 40, WINDOW, far_left, far_right)
-
-    @pl.when(is_hub)
-    def _():
-        transfers(all_tails, TAIL).wait_recv()
-
-    @pl.when(is_hub)
-    def _():
-        for ch in range(4):
-            total = tails_in[wrap_from, ch]
-            for j in range(wrap_from + 1, n):
-                total = total + tails_in[j, ch]
-            fh[ch, pl.ds(PAD, 4), :] = tail_zero[ch, pl.ds(0, 4), :]
-            fh[ch, pl.ds(PAD + 12, 4), :] = from_left[0, ch, pl.ds(4, 4), :]
-            for r in range(2, rows_dev):
-                half = (r % 2) * 4
-                fh[ch, pl.ds(PAD + 12 * r, 4), :] = total[half : half + 4]
-            for r in range(rows_dev):
-                fh[ch, pl.ds(PAD + 12 * r + 4, 8), :] = zs[ch * 4 + r, pl.ds(PAD, 8), :]
-        for r in range(rows_dev):
-            seam_owner[r, :, :] = zs[16 + r, pl.ds(PAD, 8), :]
-
-    @pl.when(has_left)
-    def _():
-        for r in range(rows_dev):
-            for ch in range(5):
-                window = z_window[r, ch]
-                if r >= 2:
-                    window = window + jnp.where(far_left, w_left[r - 2, ch], 0.0)
-                    window = window + jnp.where(far_right, w_right[r - 2, ch], 0.0)
-                if ch == 4:
-                    seam_owner[r, pl.ds(0, 4), :] = window[4:8]
-                    continue
-                base = PAD + 12 * r
-                fh[ch, pl.ds(base, 8), :] = window
-                fh[ch, pl.ds(base + 8, 4), :] = heads[r // 2, ch, pl.ds((r % 2) * 4, 4), :]
-
-    merid = PAD + 12 * rows_dev
     for r in range(rows_dev):
         take = (r % 2) * 4
         for ch in range(4):
             turned = ch if ch == 3 else 2 - ch
             sign = -1.0 if ch == 3 else 1.0
-            base = merid + r * 24
+            base = PAD + r * 24
             for j in range(4):
                 plain = m_halo[0, r // 2, ch, pl.ds(take + j, 1), :]
                 pole = sign * m_halo[0, r // 2, turned, pl.ds(take + 3 - j, 1), :]
@@ -572,46 +539,62 @@
             fh[ch, pl.ds(base + 4, 8), :] = ms[ch * 4 + r, pl.ds(PAD, 8), :]
             fh[ch, pl.ds(base + 12, 8), :] = ms[ch * 4 + r, pl.ds(PAD + cells - 8, 8), :]
 
-    def wanted(r):
-        at = pl.ds(PAD + 12 * r + 4, 4)
-        return fh[0, at, :] + fh[1, at, :] + fh[2, at, :]
-
-    seam_before = [wanted(r) for r in range(rows_dev)]
-    advance_strips(fh, fh1, products, weights, 36 * rows_dev, 48)
+    advance_strips(fh, fh1, products, weights, 24 * rows_dev, 48)
     for r in range(rows_dev):
         for w in range(3):
-            at, base = w * 4 + r, merid + r * 24
+            at, base = w * 4 + r, PAD + r * 24
             ms2[at, pl.ds(PAD, 4), :] = fh[w, pl.ds(base + 4, 4), :]
             ms2[at, pl.ds(PAD + cells - 4, 4), :] = fh[w, pl.ds(base + 16, 4), :]
 
+    @pl.when(plain_far)
+    def _():
+        transfers(32, HEAD).wait_recv()
+
+    @pl.when(ends_here)
+    def _():
+        transfers(64, HEAD).wait_recv()
+
+    beside((rows_dev - 2) * 40, WINDOW, far_left, far_right)
+
     @pl.when(is_hub)
     def _():
+        transfers(all_tails, TAIL).wait_recv()
+
+    own_base = (me * GLON_DEV + 1).astype(F32)
+    for r in range(rows_dev):
+        end = jnp.where(is_hub, 4, lengths[r] - start)
+        seam_room[r, :, :] = jnp.full((8, 128), end, jnp.int32).astype(F32)
+
+    @pl.when(is_hub)
+    def _():
+        for ch in range(4):
+            total = tails_in[wrap_from, ch]
+            for j in range(wrap_from + 1, n):
+                total = total + tails_in[j, ch]
+            fz[ch, pl.ds(PAD, 4), :] = tail_zero[ch, pl.ds(0, 4), :]
+            fz[ch, pl.ds(PAD + 12, 4), :] = from_left[0, ch, pl.ds(4, 4), :]
+            for r in range(2, rows_dev):
+                half = (r % 2) * 4
+                fz[ch, pl.ds(PAD + 12 * r, 4), :] = total[half : half + 4]
+            for r in range(rows_dev):
+                fz[ch, pl.ds(PAD + 12 * r + 4, 8), :] = zs[ch * 4 + r, pl.ds(PAD, 8), :]
         for r in range(rows_dev):
-            for w in range(3):
-                zs2[w * 4 + r, pl.ds(PAD, 4), :] = fh[w, pl.ds(PAD + 12 * r + 4, 4), :]
+            seam_owner[r, :, :] = zs[16 + r, pl.ds(PAD, 8), :] - own_base
 
     @pl.when(has_left)
     def _():
         for r in range(rows_dev):
-            for block in range(0, cells, 8):
-                ahead = block - (lengths[r] - start)
-                inside = (index8 + ahead >= -4) & (index8 + ahead < 0)
-                take = PAD + 12 * r + 8 + jnp.clip(ahead, -12, 0)
-                for w in range(3):
-                    at = w * 4 + r
-                    old = zs2[at, pl.ds(PAD + block, 8), :]
-                    zs2[at, pl.ds(PAD + block, 8), :] = jnp.where(
-                        inside, fh[w, pl.ds(take, 8), :], old
-                    )
-
-    for r in range(rows_dev):
-        delta = (wanted(r) - seam_before[r]) * scale
-        owner = seam_owner[r, pl.ds(0, 4), :]
-        for g in range(GLON_DEV):
-            mine = owner == (me * GLON_DEV + g + 1).astype(F32)
-            co_ref[g, pl.ds(r, 1), :] += jnp.sum(
-                jnp.where(mine, delta, 0.0), axis=0, keepdims=True
-            )
+            for ch in range(5):
+                window = z_window[r, ch]
+                if r >= 2:
+                    window = window + jnp.where(far_left, w_left[r - 2, ch], 0.0)
+                    window = window + jnp.where(far_right, w_right[r - 2, ch], 0.0)
+                if ch == 4:
+                    seam_owner[r, pl.ds(0, 4), :] = window[4:8] - own_base
+                    continue
+                base = PAD + 12 * r
+                fz[ch, pl.ds(base, 8), :] = window
+                fz[ch, pl.ds(base + 8, 4), :] = heads[r // 2, ch, pl.ds((r % 2) * 4, 4), :]
 
     beside(8, PART, has_left, has_right)
 
@@ -642,19 +625,61 @@
             transfers(count, sem).wait_send()
 
 
-def finish(cells, rows_dev, zs, ms, co, zo_hbm, mo_hbm, co_hbm, zo, mo, sems):
-    copies = [pltpu.make_async_copy(co, co_hbm, sems.at[6])]
-    copies[0].start()
-    for i, (state, staged, out) in enumerate(((ms, mo, mo_hbm), (zs, zo, zo_hbm))):
-        for w in range(3):
-            rows = staged.at[w].reshape(128 * rows_dev, cells)
-            for r in range(rows_dev):
-                block = state[w * 4 + r, pl.ds(PAD, cells), :]
-                rows[pl.ds(r, 128, stride=rows_dev), :] = block.T
-            copies.append(
-                pltpu.make_async_copy(staged.at[w], out.at[:, w], sems.at[3 * i + w])
+def finish(
+    cells, rows_dev,
+    zs, ms, co_in, fz, seam_owner, seam_room, weights,
+    zo_hbm, mo_hbm, co_hbm,
+    zo, mo, co, f1, f2, products, sems,
+):
+    rows = 12 * rows_dev
+    index8 = lax.broadcasted_iota(jnp.int32, (8, 128), 0)
+    copies = []
+
+    def write(blocks, staged, out, w, sem):
+        lines = staged.at[w].reshape(128 * rows_dev, cells)
+        for r in range(rows_dev):
+            lines[pl.ds(r, 128, stride=rows_dev), :] = blocks(w, r).T
+        copies.append(pltpu.make_async_copy(staged.at[w], out.at[:, w], sems.at[sem]))
+        copies[-1].start()
+
+    def wanted(strips, r):
+        at = pl.ds(PAD + 12 * r + 4, 4)
+        return strips[0, at, :] + strips[1, at, :] + strips[2, at, :]
+
+    for buf in (f1, f2):
+        for ch in range(3):
+            buf[ch, pl.ds(0, PAD), :] = jnp.zeros((PAD, 128), F32)
+            buf[ch, pl.ds(PAD + rows, PAD), :] = jnp.zeros((PAD, 128), F32)
+    rooms = [jnp.max(seam_room[r]).astype(jnp.int32) for r in range(rows_dev)]
+    merid = lambda w, r: ms[w * 4 + r, pl.ds(PAD, cells), :]
+    for t, (src, dst) in enumerate(((fz, f1), (f1, f2), (f2, f1), (f1, f2))):
+        strips_substep(src, dst, fz, products, weights, rows, 48, t == SUB - 1)
+        if t < 3:
+            write(merid, mo, mo_hbm, t, t)
+
+    def zonal(w, r):
+        parts = []
+        for block in range(0, cells, 8):
+            ahead = block - rooms[r]
+            inside = (index8 + ahead >= -4) & (index8 + ahead < 0)
+            take = PAD + 12 * r + 8 + jnp.clip(ahead, -12, 0)
+            old = zs[w * 4 + r, pl.ds(PAD + block, 8), :]
+            parts.append(jnp.where(inside, f2[w, pl.ds(take, 8), :], old))
+        return jnp.concatenate(parts, axis=0)
+
+    for w in range(3):
+        write(zonal, zo, zo_hbm, w, 3 + w)
+    scale = GLON_DEV / (3.0 * cells)
+    for r in range(rows_dev):
+        delta = (wanted(f2, r) - wanted(fz, r)) * scale
+        owner = seam_owner[r, pl.ds(0, 4), :]
+        for g in range(GLON_DEV):
+            mine = jnp.where(owner == float(g), delta, 0.0)
+            co[g, pl.ds(r, 1), :] = co_in[g, pl.ds(r, 1), :] + jnp.sum(
+                mine, axis=0, keepdims=True
             )
-            copies[-1].start()
+    copies.append(pltpu.make_async_copy(co, co_hbm, sems.at[6]))
+    copies[-1].start()
     for done in copies:
         done.wait()
 
@@ -671,7 +696,8 @@
         hbm = pl.BlockSpec(memory_space=pltpu.HBM)
         shape = jax.ShapeDtypeStruct
         state = (16, cells + 2 * PAD, 128)
-        strips = (4, 32 * rows_dev + 2 * PAD, 128)
+        strips = (4, 24 * rows_dev + 2 * PAD, 128)
+        seam = (4, 12 * rows_dev + 2 * PAD, 128)
         packet = pltpu.VMEM((2, 4, 8, 128), F32)
         small = pltpu.VMEM((8, 128), F32)
         products = pltpu.VMEM((rows_dev * 3 * cells, 128), F32)
@@ -682,9 +708,12 @@
             out_shape=(
                 shape(state, F32), shape(state, F32),
                 shape((GLON_DEV, rows_dev, nv * lev), F32),
+                shape(seam, F32),
+                shape((rows_dev, 8, 128), F32), shape((rows_dev, 8, 128), F32),
+                shape((256, 256), jnp.bfloat16),
             ),
             in_specs=[hbm] * 7,
-            out_specs=(vmem,) * 3,
+            out_specs=(vmem,) * 7,
             scratch_shapes=[
                 pltpu.SMEM((rows_dev,), jnp.int32),
                 pltpu.VMEM((nv * lev * wid, 2, rows_dev // 2, cells), F32),
@@ -695,10 +724,10 @@
                 pltpu.VMEM((nv * lev, lev), F32),
                 pltpu.VMEM((20, *state[1:]), F32), pltpu.VMEM(state, F32),
                 pltpu.VMEM(state, F32), pltpu.VMEM(state, F32),
-                pltpu.VMEM((4, 36 * rows_dev + 2 * PAD, 128), F32),
-                pltpu.VMEM((4, 36 * rows_dev + 2 * PAD, 128), F32),
+                pltpu.VMEM(strips, F32),
+                pltpu.VMEM(strips, F32),
                 pltpu.VMEM(strips, F32), pltpu.VMEM(strips, F32),
-                products, pltpu.VMEM((256, 256), jnp.bfloat16),
+                products,
                 packet, packet, pltpu.VMEM((3, 4, 8, 128), F32), packet, packet,
                 packet, packet, packet,
                 pltpu.VMEM((n, 4, 8, 128), F32),
@@ -707,7 +736,6 @@
                 pltpu.VMEM((rows_dev, 5, 8, 128), F32),
                 pltpu.VMEM((rows_dev - 2, 5, 8, 128), F32),
                 pltpu.VMEM((rows_dev - 2, 5, 8, 128), F32),
-                pltpu.VMEM((rows_dev, 8, 128), F32),
                 small, small, small, small,
                 dma((8,)), dma((6,)),
                 regular((2,)), regular((2,)), regular((4,)),
@@ -736,12 +764,13 @@
                 shape((nv * lev, wid, rows_dev, cells), F32),
                 shape((GLON_DEV, rows_dev, nv * lev), F32),
             ),
-            in_specs=[vmem] * 3,
+            in_specs=[vmem] * 7,
             out_specs=(hbm,) * 3,
             scratch_shapes=[
                 pltpu.VMEM((wid, nv * lev, rows_dev, cells), F32),
                 pltpu.VMEM((wid, nv * lev, rows_dev, cells), F32),
-                dma((7,)),
+                pltpu.VMEM((GLON_DEV, rows_dev, nv * lev), F32),
+                pltpu.VMEM(seam, F32), pltpu.VMEM(seam, F32), products, dma((7,)),
             ],
             compiler_params=pltpu.CompilerParams(vmem_limit_bytes=40 * 1024 * 1024),
         )(*held)

time: 12 us -> 11.9 us (level)
  the two profiles are of different devices: /device:TPU:0 before, /device:TPU:7 now
where the time goes in v5:
time: 11.9 us; the launch traced here: 11.8 us
  Pallas kernels  11.2 us (94%)
  between operations  0.64 us (5%)
    pallas_call x1, Pallas kernels, shards(): pl.pallas_call(functools.partial(kernel, n, n_lat, cells, rows_dev), out_...  9.45 us
    pallas_call x1, Pallas kernels, shards(): pl.pallas_call(functools.partial(finish, cells, rows_dev), out_shape=(sha...  1.7 us

profile of v5, /device:TPU:7, one launch (start us, length us, event | category | flops | bytes accessed | tf_op | source)
XLA Modules:
  0.0 11.8 jit_solution(6970751764262439938)
XLA Ops:
  0.6 9.5 %shard_map.94 = (f32[16,144,128]{2,1,0:T(8,128)S(1)}, f32[16,144,128]{2,1,0:T(8,128)S(1)}, f32[4,4,128]{2,1,0:T(4,128)S(1)}, f32[4,64,128]{2,1,0:T(8,128)S(1)}, ...) custom-call(s32[4]{0:T(128)} %len_hbm.1, f32[384,2,2,128]{3,2,1,0:T(2,128)} %bitcast.7, ...), custom_call_target="tpu_custom_call" | custom-call | tf_op jit(solution)/shard_map/pallas_call | solution.py:706
  10.1 1.7 %shard_map.95 = (f32[128,3,4,128]{3,2,1,0:T(4,128)}, f32[128,3,4,128]{3,2,1,0:T(4,128)}, f32[4,4,128]{2,1,0:T(4,128)}) custom-call(f32[16,144,128]{2,1,0:T(8,128)S(1)} %get-tuple-element.13.zs, f32[16,144,128]{2,1,0:T(8,128)S(1)} %get-tuple-element.14.ms, f32[4,4,128]{2,1,0:T(4,128)S(1)} %get-tuple-element.15.co_in, f32[4,64,128]{2,1,0:T(8,128)S(1)} %get-tuple-element.16.fz, ...), custom_call_target="tpu_custom_call" | custom-call | tf_op jit(solution)/shard_map/pallas_call | solution.py:760

commit v6 on v5

--- a/solution.py
+++ b/solution.py
@@ -654,8 +654,9 @@
     merid = lambda w, r: ms[w * 4 + r, pl.ds(PAD, cells), :]
     for t, (src, dst) in enumerate(((fz, f1), (f1, f2), (f2, f1), (f1, f2))):
         strips_substep(src, dst, fz, products, weights, rows, 48, t == SUB - 1)
-        if t < 3:
-            write(merid, mo, mo_hbm, t, t)
+        if t == 0:
+            for w in range(3):
+                write(merid, mo, mo_hbm, w, w)
 
     def zonal(w, r):
         parts = []

time: 11.9 us -> 11.9 us (level)
  the two profiles are of different devices: /device:TPU:7 before, /device:TPU:3 now
where the time goes in v6:
time: 11.9 us; the launch traced here: 11.8 us
  Pallas kernels  11.2 us (94%)
  between operations  0.64 us (5%)
    pallas_call x1, Pallas kernels, shards(): pl.pallas_call(functools.partial(kernel, n, n_lat, cells, rows_dev), out_...  9.45 us
    pallas_call x1, Pallas kernels, shards(): pl.pallas_call(functools.partial(finish, cells, rows_dev), out_shape=(sha...  1.7 us

profile of v6, /device:TPU:3, one launch (start us, length us, event | category | flops | bytes accessed | tf_op | source)
XLA Modules:
  0.0 11.8 jit_solution(6970751764262439938)
XLA Ops:
  0.6 9.5 %shard_map.94 = (f32[16,144,128]{2,1,0:T(8,128)S(1)}, f32[16,144,128]{2,1,0:T(8,128)S(1)}, f32[4,4,128]{2,1,0:T(4,128)S(1)}, f32[4,64,128]{2,1,0:T(8,128)S(1)}, ...) custom-call(s32[4]{0:T(128)} %len_hbm.1, f32[384,2,2,128]{3,2,1,0:T(2,128)} %bitcast.7, ...), custom_call_target="tpu_custom_call" | custom-call | tf_op jit(solution)/shard_map/pallas_call | solution.py:707
  10.1 1.7 %shard_map.95 = (f32[128,3,4,128]{3,2,1,0:T(4,128)}, f32[128,3,4,128]{3,2,1,0:T(4,128)}, f32[4,4,128]{2,1,0:T(4,128)}) custom-call(f32[16,144,128]{2,1,0:T(8,128)S(1)} %get-tuple-element.13.zs, f32[16,144,128]{2,1,0:T(8,128)S(1)} %get-tuple-element.14.ms, f32[4,4,128]{2,1,0:T(4,128)S(1)} %get-tuple-element.15.co_in, f32[4,64,128]{2,1,0:T(8,128)S(1)} %get-tuple-element.16.fz, ...), custom_call_target="tpu_custom_call" | custom-call | tf_op jit(solution)/shard_map/pallas_call | solution.py:761
